TPU v7x, 32 devices: a whole 2x2x4 slice. The times are simulated.
32 devices in a mesh: shot: 8 (over z, y), grp: 4 (over x, core).
Axes of the slice: x: 2, y: 2, z: 4, core: 2. Of those that a mesh axis runs over, the one named last changes fastest.
Arguments:
- offsets: bfloat16 [6144, 32, 512], P(('shot', 'grp')), may hold values from -500 to 500
- slant_weights: bfloat16 [64, 32], replicated, may hold values from -1 to 1
- live: int32 [6144, 64], P(('shot', 'grp')), may hold values from 0 to 1, as said below
- block_tile: int32 [3072, 1], P(('shot', 'grp')), may hold values from 0 to 7; in each aligned block of 96 rows (0 to 95, 96 to 191, ...) at most 13 rows name the same one
- image_slot: int32 [3072], P(('shot', 'grp')), may hold values from 0 to 15
Outputs:
- image: bfloat16 [128, 128, 512], P(('shot', 'grp'))
Inputs may be any that keep to these rules, and one draw needn't show every extreme that they name: Each position's live angles are 0 up to a cutoff minus 1, the cutoff at least 16; the first position of every 192 positions keeps all 64 angles. `block_tile`: among the 96 blocks of one device no tile is named more than 13 times.
All inputs are finite; a program needn't handle non-finite values.
Results may differ from a plain program's by a relative error of at most 0.0049.
Values may be sent and summed in bfloat16 or wider, within the bound.
A program may use at most 192 MiB of HBM per device.

v0:
```python
import functools

import jax
import jax.numpy as jnp
from jax import lax
from jax.experimental import pallas as pl
from jax.experimental.pallas import tpu as pltpu
from jax.sharding import PartitionSpec as P

IMG_DEV = 4
PAIR = 2
LANES = 128
UNROLL = 8
MESH = pl.DeviceIdType.MESH


def place(grp):
    shot, g = lax.axis_index("shot"), lax.axis_index("grp")
    return lax.div(shot, PAIR), lax.rem(shot, PAIR) * grp + g


def at(plane, spot, grp):
    return (plane * PAIR + lax.div(spot, grp), lax.rem(spot, grp))


def share(spot, width, depth):
    start = spot * width
    return lax.div(start, depth), pl.multiple_of(lax.rem(start, depth), LANES)


def relative(spot, grp, r):
    mid = grp // 2
    pair, rest = lax.div(spot, grp), lax.rem(spot, grp)
    m, c = lax.div(rest, 2), lax.rem(rest, 2)
    rp, rm, rc = r // grp, (r % grp) // 2, r % 2
    pair, m, c = lax.rem(pair + rp, PAIR), lax.rem(m + rm, mid), lax.rem(c + rc, 2)
    return (pair * mid + m) * 2 + c


def orders(grp):
    size = PAIR * grp
    far = list(range(grp + 2, size))
    side = list(range(grp, grp + 2))
    ahead = list(range(2, grp))
    turn = []
    for i in range(max(len(far), len(ahead))):
        for group in (far, side, ahead):
            turn += group[i : i + 1]
    return [1] + turn


def exchange_kernel(
    grp, off, aux, w_in, part, mom, w, raw, aux_in, codes, acc, seg, send, recv, asend, arecv, lsem
):
    size = PAIR * grp
    plane, spot = place(grp)
    blocks, depth, width = off.shape[0], off.shape[3], raw.shape[3]
    angles, images = w.shape[1], acc.shape[0]
    j, first = share(spot, width, depth)
    mine = pltpu.make_async_copy(off.at[:, j, :, pl.ds(first, width)], raw.at[0], lsem.at[0])
    mine.start()
    own_codes = pltpu.make_async_copy(aux, codes.at[0], lsem.at[1])
    own_codes.start()
    weigh = pltpu.make_async_copy(w_in, w, lsem.at[size + 1])
    weigh.start()
    barrier = pltpu.get_barrier_semaphore()
    for r in range(1, size):
        pl.semaphore_signal(
            barrier, inc=1, device_id=at(plane, relative(spot, grp, r), grp), device_id_type=MESH
        )
    pl.semaphore_wait(barrier, size - 1)
    data, notes = {}, {}
    for r in orders(grp):
        peer = relative(spot, grp, r)
        pj, pfirst = share(peer, width, depth)
        dev = at(plane, peer, grp)
        notes[r] = pltpu.make_async_remote_copy(
            src_ref=aux,
            dst_ref=aux_in.at[r],
            send_sem=asend.at[r - 1],
            recv_sem=arecv.at[r - 1],
            device_id=dev,
            device_id_type=MESH,
        )
        data[r] = pltpu.make_async_remote_copy(
            src_ref=off.at[:, pj, :, pl.ds(pfirst, width)],
            dst_ref=raw.at[r],
            send_sem=send.at[r - 1],
            recv_sem=recv.at[r - 1],
            device_id=dev,
            device_id_type=MESH,
        )
    for r in orders(grp):
        notes[r].start()
    for r in orders(grp):
        data[r].start()

    acc[...] = jnp.zeros_like(acc)
    seg[blocks] = jnp.zeros((angles, width), jnp.float32)
    row = lax.broadcasted_iota(jnp.int32, (angles, width), 0)
    weigh.wait()
    weights = w[...].astype(jnp.float32).T.astype(jnp.bfloat16)
    square = jnp.zeros((angles, width), jnp.float32)
    count = jnp.zeros((angles, width), jnp.float32)
    for r in [0] + orders(grp):
        if r:
            notes[r].wait()
            code = pltpu.make_async_copy(aux_in.at[r], codes.at[r], lsem.at[r + 1])
            code.start()
            code.wait()
            data[r].wait()
        else:
            own_codes.wait()
            mine.wait()

        def slant(i, carry, r=r):
            square, count = carry
            start = i * UNROLL
            x = jnp.concatenate([raw[r, start + t] for t in range(UNROLL)], axis=1)
            y = jnp.dot(weights, x, preferred_element_type=jnp.float32)
            for t in range(UNROLL):
                alive = row < codes[r, 1 + j, start + t]
                slanted = jnp.where(alive, y[:, t * width : (t + 1) * width], 0.0)
                slanted = slanted.astype(jnp.bfloat16).astype(jnp.float32)
                square += slanted * slanted
                count += jnp.where(alive, 1.0, 0.0)
                seg[start + t] = slanted + seg[codes[r, 0, start + t]]
            return square, count

        square, count = lax.fori_loop(0, blocks // UNROLL, slant, (square, count))

        def stack(i, _, r=r):
            start = i * UNROLL
            line, column = lax.div(start, LANES), lax.rem(start, LANES)
            for t in range(UNROLL):
                acc[start + t] += seg[codes[r, 3 + line, column + t]]
            return 0

        lax.fori_loop(0, images // UNROLL, stack, 0)

    def narrow(i, _):
        start = pl.multiple_of(i * UNROLL, UNROLL)
        part[pl.ds(start, UNROLL)] = acc[pl.ds(start, UNROLL)].astype(jnp.bfloat16)
        return 0

    lax.fori_loop(0, images // UNROLL, narrow, 0)
    lane = lax.broadcasted_iota(jnp.int32, (angles, LANES), 1)
    square = jnp.sum(square, axis=1, keepdims=True)
    count = jnp.sum(count, axis=1, keepdims=True)
    both = jnp.where(lane == 0, square, jnp.where(lane == 1, count, 0.0))
    both = jnp.concatenate([both, jnp.zeros((LANES - angles, LANES), jnp.float32)], axis=0)
    mom[...] = both.T[: mom.shape[0]]


def gather_kernel(
    grp, part, mom, out, held, total, fin, pin, qin, half_sum, zs, zr, ps, pr, qs, qr, fs, fr, lsem
):
    size = PAIR * grp
    planes = held.shape[1] + 1
    plane, spot = place(grp)
    pieces, rows, angles, width = held.shape[2:]
    depth = out.shape[2]
    chunk = pieces * rows
    lower = jnp.where(plane < planes // 2, 1, 0)
    barrier = pltpu.get_barrier_semaphore()
    for r in range(1, size):
        pl.semaphore_signal(
            barrier, inc=1, device_id=at(plane, lax.rem(spot + r, size), grp), device_id_type=MESH
        )
    for r in range(1, planes):
        pl.semaphore_signal(
            barrier, inc=1, device_id=at(lax.rem(plane + r, planes), spot, grp), device_id_type=MESH
        )
    pl.semaphore_wait(barrier, size + planes - 2)

    def along(up):
        spot_on_line = plane * up + (planes - 1 - plane) * (1 - up)
        following = lax.rem(plane + 2 * up - 1 + planes, planes)
        return 1 - up, spot_on_line, following

    def rows_of(up, s, h):
        target = (planes - 1 - s) * up + s * (1 - up)
        return target * chunk + h * rows

    def hop(up, s, h, source):
        way, _, following = along(up)
        return pltpu.make_async_remote_copy(
            src_ref=source,
            dst_ref=held.at[way, s, h],
            send_sem=zs.at[way, s, h],
            recv_sem=zr.at[way, s, h],
            device_id=at(following, spot, grp),
            device_id_type=MESH,
        )

    def begin(s):
        @pl.when(along(lower)[1] == 0)
        def _():
            for h in range(pieces):
                hop(lower, s, h, part.at[pl.ds(rows_of(lower, s, h), rows)]).start()

    def step(up, s, h):
        way, here, _ = along(up)
        end = planes - 1 - s

        @pl.when((here > 0) & (here <= end))
        def _():
            hop(up, s, h, held.at[way, s, h]).wait_recv()

        @pl.when((here > 0) & (here < end))
        def _():
            start = rows_of(up, s, h)

            def add(i, _):
                value = held[way, s, h, i].astype(jnp.float32) + part[start + i].astype(jnp.float32)
                held[way, s, h, i] = value.astype(jnp.bfloat16)
                return 0

            lax.fori_loop(0, rows, add, 0)
            hop(up, s, h, held.at[way, s, h]).start()

        @pl.when((here > 0) & (here == end))
        def _():
            def add(i, _):
                total[h * rows + i] += held[way, s, h, i].astype(jnp.float32)
                return 0

            lax.fori_loop(0, rows, add, 0)

    def finish(up, s, h):
        way, here, _ = along(up)

        @pl.when(here < planes - 1 - s)
        def _():
            hop(up, s, h, held.at[way, s, h]).wait_send()

    near = [
        pltpu.make_async_remote_copy(
            src_ref=mom,
            dst_ref=pin.at[r - 1],
            send_sem=ps.at[r - 1],
            recv_sem=pr.at[r - 1],
            device_id=at(plane, lax.rem(spot + r, size), grp),
            device_id_type=MESH,
        )
        for r in range(1, size)
    ]
    for copy in near:
        copy.start()
    begin(0)
    total[...] = part[pl.ds(plane * chunk, chunk)].astype(jnp.float32)
    moments = mom[...]
    for copy in near:
        copy.wait()
    for r in range(1, size):
        moments += pin[r - 1]
    half_sum[...] = moments
    wide = [
        pltpu.make_async_remote_copy(
            src_ref=half_sum,
            dst_ref=qin.at[r - 1],
            send_sem=qs.at[r - 1],
            recv_sem=qr.at[r - 1],
            device_id=at(lax.rem(plane + r, planes), spot, grp),
            device_id_type=MESH,
        )
        for r in range(1, planes)
    ]
    for copy in wide:
        copy.start()
    for s in range(1, planes - 1):
        begin(s)
    for s in range(planes - 1):
        for up in (lower, 1 - lower):
            for h in range(pieces):
                step(up, s, h)
    for copy in wide:
        copy.wait()
    moments = half_sum[...]
    for r in range(1, planes):
        moments += qin[r - 1]
    gain = lax.rsqrt(moments[0:1] / moments[1:2] + 1e-06)
    gain = jnp.broadcast_to(gain, (LANES, LANES)).T[:angles]

    def body(i, _):
        fin[i] = (total[i] * gain).astype(jnp.bfloat16)
        return 0

    lax.fori_loop(0, chunk, body, 0)

    each = chunk // size
    j, first = share(spot, width, depth)
    view = out.at[:, pl.ds(pl.multiple_of(j * angles, angles), angles), pl.ds(first, width)]
    last = pltpu.make_async_copy(fin.at[pl.ds(spot * each, each)], view, lsem.at[1])
    final = []
    for r in range(1, size):
        peer = lax.rem(spot + r, size)
        final.append(
            pltpu.make_async_remote_copy(
                src_ref=fin.at[pl.ds(peer * each, each)],
                dst_ref=view,
                send_sem=fs.at[r - 1],
                recv_sem=fr.at[r - 1],
                device_id=at(plane, peer, grp),
                device_id_type=MESH,
            )
        )
    for copy in final:
        copy.start()
    last.start()
    last.wait()
    for copy in final:
        copy.wait()
    for s in range(planes - 1):
        for up in (lower, 1 - lower):
            for h in range(pieces):
                finish(up, s, h)


def local(offsets, slant_weights, live, block_tile, image_slot):
    shots, grp = lax.axis_size("shot"), lax.axis_size("grp")
    planes, size = shots // PAIR, PAIR * grp
    blocks = block_tile.shape[0]
    hs, depth = offsets.shape[1:]
    angles = slant_weights.shape[0]
    width = 2 * depth // size
    tile_rows = IMG_DEV * grp
    images = shots * tile_rows
    per_plane = images // planes
    any_space = pl.BlockSpec(memory_space=pl.ANY)
    vmem = pl.BlockSpec(memory_space=pltpu.VMEM)
    dma = pltpu.SemaphoreType.DMA

    cutoff = jnp.sum(live.reshape(blocks, 2, angles), axis=2)
    image = block_tile[:, 0] * tile_rows + image_slot
    index = jnp.arange(blocks, dtype=jnp.int32)
    same = (image[:, None] == image[None, :]) & (index[None, :] < index[:, None])
    before = jnp.max(jnp.where(same, index[None, :], -1), axis=1)
    found = image[None, :] == jnp.arange(images, dtype=jnp.int32)[:, None]
    final = jnp.max(jnp.where(found, index[None, :], -1), axis=1)
    final = jnp.where(final < 0, blocks, final).reshape(images // LANES, LANES)
    before = jnp.where(before < 0, blocks, before)
    aux = jnp.concatenate([before[None], cutoff.T], axis=0)
    aux = jnp.concatenate([jnp.pad(aux, ((0, 0), (0, LANES - blocks))), final], axis=0)
    aux = jnp.pad(aux, ((0, -aux.shape[0] % 8), (0, 0)))

    part, mom = pl.pallas_call(
        functools.partial(exchange_kernel, grp),
        out_shape=(
            jax.ShapeDtypeStruct((images, angles, width), jnp.bfloat16),
            jax.ShapeDtypeStruct((8, LANES), jnp.float32),
        ),
        in_specs=[any_space, vmem, any_space],
        out_specs=(vmem, vmem),
        scratch_shapes=[
            pltpu.VMEM((hs, angles), jnp.bfloat16),
            pltpu.VMEM((size, blocks, hs, width), jnp.bfloat16),
            pltpu.VMEM((size,) + aux.shape, jnp.int32),
            pltpu.SMEM((size,) + aux.shape, jnp.int32),
            pltpu.VMEM((images, angles, width), jnp.float32),
            pltpu.VMEM((blocks + 1, angles, width), jnp.float32),
            dma((size - 1,)),
            dma((size - 1,)),
            dma((size - 1,)),
            dma((size - 1,)),
            dma((size + 2,)),
        ],
        compiler_params=pltpu.CompilerParams(
            collective_id=0, has_side_effects=True, vmem_limit_bytes=62 * 1024 * 1024
        ),
        name="exchange",
    )(offsets.reshape(blocks, 2, hs, depth), aux, slant_weights.T)

    moments = (8, LANES)
    pieces = 4
    lines = (2, planes - 1, pieces)
    return pl.pallas_call(
        functools.partial(gather_kernel, grp),
        out_shape=jax.ShapeDtypeStruct((IMG_DEV, 2 * angles, depth), jnp.bfloat16),
        in_specs=[vmem, vmem],
        out_specs=any_space,
        scratch_shapes=[
            pltpu.VMEM(lines + (per_plane // pieces, angles, width), jnp.bfloat16),
            pltpu.VMEM((per_plane, angles, width), jnp.float32),
            pltpu.VMEM((per_plane, angles, width), jnp.bfloat16),
            pltpu.VMEM((size - 1,) + moments, jnp.float32),
            pltpu.VMEM((planes - 1,) + moments, jnp.float32),
            pltpu.VMEM(moments, jnp.float32),
            dma(lines),
            dma(lines),
            dma((size - 1,)),
            dma((size - 1,)),
            dma((planes - 1,)),
            dma((planes - 1,)),
            dma((size - 1,)),
            dma((size - 1,)),
            dma((2,)),
        ],
        compiler_params=pltpu.CompilerParams(
            collective_id=1, has_side_effects=True, vmem_limit_bytes=60 * 1024 * 1024
        ),
        name="gather",
    )(part, mom)


def solution(mesh):
    placed = (
        P(("shot", "grp"), None, None),
        P(),
        P(("shot", "grp"), None),
        P(("shot", "grp"), None),
        P(("shot", "grp")),
    )
    return jax.shard_map(
        local, mesh=mesh, in_specs=placed, out_specs=P(("shot", "grp"), None, None), check_vma=False
    )
```

profile of v0, /device:TPU:9, one launch (start us, length us, event | category | flops | bytes accessed | tf_op | source)
XLA Modules:
  0.0 134.2 jit_solution(10829901137267418051)
XLA Ops:
  0.0 0.7 bitcast_add_fusion
  0.7 0.2 select_reduce_fusion.1
  0.9 0.1 select_reduce_fusion
  1.0 0.9 reduce_sum.11
  1.8 0.1 reduce_sum.12
  2.0 0.1 copy.7
  2.1 0.6 pad.9.aux
  2.7 81.0 %exchange.1 = (bf16[128,64,128]{2,1,0:T(8,128)(2,1)}, f32[8,128]{1,0:T(8,128)}) custom-call(bf16[96,2,32,512]{3,2,1,0:T(8,128)(2,1)} %bitcast.9, s32[8,128]{1,0:T(8,128)} %pad.9.aux, bf16[32,64]{1,0:T(8,128)(2,1)} %bitcast.10), custom_call_target="tpu_custom_call" | custom-call | tf_op jit(solution)/shard_map/exchange/pallas_call | solution.py:347
  83.7 48.6 %gather.1 = bf16[4,128,512]{2,1,0:T(8,128)(2,1)} custom-call(bf16[128,64,128]{2,1,0:T(8,128)(2,1)} %get-tuple-element.7.part, f32[8,128]{1,0:T(8,128)} %get-tuple-element.8.mom), custom_call_target="tpu_custom_call" | custom-call | tf_op jit(solution)/shard_map/gather/pallas_call | solution.py:377
  132.3 1.9 %copy.9 = bf16[4,128,512]{2,1,0:T(8,128)(2,1)} copy(bf16[4,128,512]{2,1,0:T(8,128)(2,1)} %gather.1) | data formatting | bytes 1048576
  (4 shorter events, 0.0 us)
where the time goes:
time: 134 us
  Pallas kernels  130 us (97%)
  local copies, waits for them, and re-layouts  2.67 us (2%)
  other arithmetic  1.86 us (1%)
    pallas_call x1, Pallas kernels, local(): pl.pallas_call(functools.partial(exchange_kernel, grp), out_shape=(jax.Sh...  81 us
    pallas_call x1, Pallas kernels, local(): pl.pallas_call(functools.partial(gather_kernel, grp), out_shape=jax.Shape...  48.6 us

commit v1 on v0

--- a/solution.py
+++ b/solution.py
@@ -1,4 +1,5 @@
 import functools
+import math
 
 import jax
 import jax.numpy as jnp
@@ -12,6 +13,7 @@
 LANES = 128
 UNROLL = 8
 MESH = pl.DeviceIdType.MESH
+VMEM_LIMIT = 62 * 1024 * 1024
 
 
 def place(grp):
@@ -317,7 +319,7 @@
                 finish(up, s, h)
 
 
-def local(offsets, slant_weights, live, block_tile, image_slot):
+def staged(offsets, slant_weights, live, block_tile, image_slot):
     shots, grp = lax.axis_size("shot"), lax.axis_size("grp")
     planes, size = shots // PAIR, PAIR * grp
     blocks = block_tile.shape[0]
@@ -403,6 +405,521 @@
     )(part, mom)
 
 
+def round_up(value, unit):
+    return -(-value // unit) * unit
+
+
+def flip(value, bit):
+    return value + bit - 2 * value * bit
+
+
+def fused_kernel(
+    shape, off, live, tile, slot, w_in, out,
+    raw, wb, onehot, mine, theirs, cuts, squares, sl, own, part, rx1, rxv, held, ft, fin,
+    mom, sums, pin, gains,
+    in_sem, core_s, core_r, meta_s, meta_r, s1s, s1r, vs, vr, zs, zr, fs, fr, fl, ms, mr,
+):
+    planes, grp, kinds = shape
+    shot, g = lax.axis_index("shot"), lax.axis_index("grp")
+    z, y = lax.div(shot, PAIR), lax.rem(shot, PAIR)
+    x, c = lax.div(g, 2), lax.rem(g, 2)
+    blocks, hs, depth = raw.shape[1:]
+    angles = live.shape[0]
+    images = onehot.shape[0]
+    img_dev = out.shape[0]
+    wide = sl.shape[2]
+    quarters = wide // LANES
+    half = sl.shape[0]
+    per = part.shape[3] * 2
+    pairs = per // 2
+    depths = depth // wide
+    halves = angles // half
+    units = half // per
+    eight = 8
+
+    def device(dz=None, fy=False, fx=False, fc=False):
+        zz = z if dz is None else dz
+        yy = 1 - y if fy else y
+        xx = 1 - x if fx else x
+        cc = 1 - c if fc else c
+        return (zz * PAIR + yy, xx * 2 + cc)
+
+    core_peer, x_peer, y_peer = device(fc=True), device(fx=True), device(fy=True)
+    first_peer = (x_peer, y_peer)
+    second_peer = (y_peer, x_peer)
+
+    own_in = [
+        pltpu.make_async_copy(
+            off.at[:, c, :, pl.ds(d * wide, wide)],
+            raw.at[0, :, :, pl.ds(d * wide, wide)],
+            in_sem.at[d],
+        )
+        for d in range(depths)
+    ]
+    for copy in own_in:
+        copy.start()
+    barrier = pltpu.get_barrier_semaphore()
+    near = [core_peer, x_peer, y_peer]
+    near += [device(dz=lax.rem(z + r, planes)) for r in range(1, planes)]
+    for peer in near:
+        pl.semaphore_signal(barrier, inc=1, device_id=peer, device_id_type=MESH)
+
+    count_rows = live[...].astype(jnp.float32)
+    live_bf = count_rows.astype(jnp.bfloat16)
+    ones = jnp.ones((angles, LANES), jnp.bfloat16)
+    spot = lax.broadcasted_iota(jnp.int32, (blocks, 2 * blocks), 1)
+    block = lax.broadcasted_iota(jnp.int32, (blocks, 2 * blocks), 0)
+
+    def cutoff(j):
+        pick = jnp.where(spot == 2 * block + j, 1.0, 0.0).astype(jnp.bfloat16)
+        flags = lax.dot_general(
+            pick, live_bf, (((1,), (1,)), ((), ())), preferred_element_type=jnp.float32
+        )
+        total = jnp.dot(flags.astype(jnp.bfloat16), ones, preferred_element_type=jnp.float32)
+        return total.astype(jnp.int32)
+
+    image = tile[...] * (img_dev * grp) + slot[...]
+    mine[0:eight] = jnp.full((eight, LANES), -1, jnp.int32)
+    mine[0:1, 0:blocks] = image
+    mine[eight : eight + blocks] = cutoff(1 - c)
+    cuts[0] = cutoff(c)
+
+    pl.semaphore_wait(barrier, len(near))
+    meta = pltpu.make_async_remote_copy(
+        src_ref=mine, dst_ref=theirs, send_sem=meta_s.at[0], recv_sem=meta_r.at[0],
+        device_id=core_peer, device_id_type=MESH,
+    )
+    core_in = [
+        pltpu.make_async_remote_copy(
+            src_ref=off.at[:, 1 - c, :, pl.ds(d * wide, wide)],
+            dst_ref=raw.at[1, :, :, pl.ds(d * wide, wide)],
+            send_sem=core_s.at[d], recv_sem=core_r.at[d],
+            device_id=core_peer, device_id_type=MESH,
+        )
+        for d in range(depths)
+    ]
+    core_in[0].start()
+    meta.start()
+    for copy in core_in[1:]:
+        copy.start()
+
+    rows = angles * eight
+    spread = lax.broadcasted_iota(jnp.int32, (rows, angles), 0)
+    which = lax.broadcasted_iota(jnp.int32, (rows, angles), 1)
+    pick = jnp.where(lax.div(spread, eight) == which, 1.0, 0.0).astype(jnp.bfloat16)
+    tall = lax.dot_general(
+        pick, w_in[...], (((1,), (1,)), ((), ())), preferred_element_type=jnp.float32
+    ).astype(jnp.bfloat16)
+    line = lax.broadcasted_iota(jnp.int32, (hs, eight * hs), 0)
+    column = lax.broadcasted_iota(jnp.int32, (hs, eight * hs), 1)
+    copies = jnp.where(lax.rem(column, hs) == line, 1.0, 0.0).astype(jnp.bfloat16)
+    full = jnp.dot(tall, copies, preferred_element_type=jnp.float32)
+    line = lax.broadcasted_iota(jnp.int32, full.shape, 0)
+    column = lax.broadcasted_iota(jnp.int32, full.shape, 1)
+    wb[...] = jnp.where(lax.rem(line, eight) == lax.div(column, hs), full, 0.0).astype(jnp.bfloat16)
+    squares[...] = jnp.zeros_like(squares)
+
+    def slant(d, h, r):
+        def body(i, _):
+            start = i * 2 * eight
+            lhs = wb[h * half * eight : (h + 1) * half * eight]
+            lanes = slice(d * wide, (d + 1) * wide)
+            alive = cuts[r, pl.ds(start, 2 * eight)]
+            a = lax.broadcasted_iota(jnp.int32, (half, 2 * eight, LANES), 0) + h * half
+            alive = alive[None] > a
+            ys = []
+            for k in range(2):
+                data = raw[r, pl.ds(start + k * eight, eight), :, lanes].reshape(eight * hs, wide)
+                ys.append(
+                    jnp.dot(lhs, data, preferred_element_type=jnp.float32).reshape(half, eight, wide)
+                )
+            total = squares[h * half : (h + 1) * half]
+            for k in range(quarters):
+                cut = slice(k * LANES, (k + 1) * LANES)
+                v = jnp.concatenate([ys[0][:, :, cut], ys[1][:, :, cut]], axis=1)
+                v = jnp.where(alive, v, 0.0)
+                q = v * v
+                total += q[:, :eight] + q[:, eight:]
+                sl[:, pl.ds(r * blocks + start, 2 * eight), cut] = v.astype(jnp.bfloat16)
+            squares[h * half : (h + 1) * half] = total
+            return 0
+
+        lax.fori_loop(0, blocks // (2 * eight), body, 0)
+
+    def stack(cu):
+        base = cu % units * per
+
+        def body(m, _):
+            ys = [
+                jnp.dot(onehot[...], sl[base + 2 * m + k], preferred_element_type=jnp.float32)
+                for k in range(2)
+            ]
+            for l in range(2):
+                p = 2 * cu + l
+                cut = slice(l * LANES, (l + 1) * LANES)
+                for t in range(planes):
+                    for ry in range(2):
+                        for rx in range(2):
+                            r = ((t * 2 + ry) * 2 + rx) * eight
+                            v = jnp.concatenate([ys[k][r : r + eight, cut] for k in range(2)], axis=0)
+                            one, two = (rx, ry) if l == 0 else (ry, rx)
+                            if one == 0:
+                                own[p, t, two, m] = v
+                            else:
+                                part[p, t, two, m] = v.astype(jnp.bfloat16)
+            return 0
+
+        lax.fori_loop(0, pairs, body, 0)
+
+    def s1(p, t):
+        return pltpu.make_async_remote_copy(
+            src_ref=part.at[p, t], dst_ref=rx1.at[p, t],
+            send_sem=s1s.at[p, t], recv_sem=s1r.at[p, t],
+            device_id=first_peer[p % 2], device_id_type=MESH,
+        )
+
+    def across(p, t, source):
+        return pltpu.make_async_remote_copy(
+            src_ref=source, dst_ref=rxv.at[p, t],
+            send_sem=vs.at[p, t], recv_sem=vr.at[p, t],
+            device_id=second_peer[p % 2], device_id_type=MESH,
+        )
+
+    def late(p):
+        return kinds[p // 2] == "vz"
+
+    def hop(p, way, s, source):
+        n = 1 if late(p) else 2
+        following = lax.rem(z + (1 if way == 0 else planes - 1), planes)
+        return pltpu.make_async_remote_copy(
+            src_ref=source, dst_ref=held.at[p, way, s, pl.ds(0, n)],
+            send_sem=zs.at[p, way, s], recv_sem=zr.at[p, way, s],
+            device_id=device(dz=following), device_id_type=MESH,
+        )
+
+    def begin(p, t):
+        n = 1 if late(p) else 2
+        if t > 0:
+            @pl.when(z == 0)
+            def _():
+                hop(p, 0, planes - 1 - t, rx1.at[p, t, pl.ds(0, n)]).start()
+        if t < planes - 1:
+            @pl.when(z == planes - 1)
+            def _():
+                hop(p, 1, t, rx1.at[p, t, pl.ds(0, n)]).start()
+
+    def start_first(cu):
+        for t in far_first(planes):
+            for l in range(2):
+                s1(2 * cu + l, t).start()
+
+    def first(cu):
+        for t in far_first(planes):
+            for l in range(2):
+                p = 2 * cu + l
+                s1(p, t).wait_recv()
+                for k in (1, 0):
+                    total = own[p, t, k] + rx1[p, t, k].astype(jnp.float32)
+                    own[p, t, k] = total
+                    rx1[p, t, k] = total.astype(jnp.bfloat16)
+                if late(p):
+                    across(p, t, rx1.at[p, t, 1]).start()
+                else:
+                    begin(p, t)
+
+    def second(cu):
+        for t in far_first(planes):
+            for l in range(2):
+                p = 2 * cu + l
+                across(p, t, rx1.at[p, t, 1]).wait_recv()
+                total = own[p, t, 0] + rxv[p, t].astype(jnp.float32)
+                own[p, t, 0] = total
+                rx1[p, t, 0] = total.astype(jnp.bfloat16)
+                begin(p, t)
+
+    def tick(cu, tau):
+        for way in range(2):
+            here = z if way == 0 else planes - 1 - z
+            s = tau - here
+            target = planes - 1 - s if way == 0 else s
+            for l in range(2):
+                p = 2 * cu + l
+                n = 1 if late(p) else 2
+
+                @pl.when((here >= 1) & (s >= 0))
+                def _(p=p, n=n, way=way, s=s, target=target):
+                    hop(p, way, s, held.at[p, way, s, pl.ds(0, n)]).wait_recv()
+                    for k in range(n):
+                        value = held[p, way, s, k].astype(jnp.float32) + own[p, target, k]
+                        if tau < planes - 1:
+                            held[p, way, s, k] = value.astype(jnp.bfloat16)
+                        else:
+                            own[p, target, k] = value
+                    if tau < planes - 1:
+                        hop(p, way, s, held.at[p, way, s, pl.ds(0, n)]).start()
+
+    def third(cu):
+        for l in range(2):
+            p = 2 * cu + l
+            rx1[p, z, 1] = own[p, z, 1].astype(jnp.bfloat16)
+            across(p, 0, rx1.at[p, z, 1]).start()
+
+    def leave(p):
+        cu, l = p // 2, p % 2
+        line = slice(cu // units % halves * half + cu % units * per, None)
+        line = slice(line.start, line.start + per)
+        lanes = (cu // (units * halves)) * wide + l * LANES
+        row = pl.multiple_of(c * angles + line.start, per)
+        view = out.at[:, pl.ds(row, per), pl.ds(lanes, LANES)]
+        send = pltpu.make_async_remote_copy(
+            src_ref=fin.at[pl.ds(img_dev, img_dev), line, pl.ds(lanes, LANES)], dst_ref=view,
+            send_sem=fs.at[p], recv_sem=fr.at[p],
+            device_id=core_peer, device_id_type=MESH,
+        )
+        keep = pltpu.make_async_copy(
+            fin.at[pl.ds(0, img_dev), line, pl.ds(lanes, LANES)], view, fl.at[p]
+        )
+        return send, keep, line, lanes
+
+    def finish(cu):
+        for l in range(2):
+            p = 2 * cu + l
+            total = own[p, z, 0]
+            if not late(p):
+                across(p, 0, rx1.at[p, z, 1]).wait_recv()
+                total += rxv[p, 0].astype(jnp.float32)
+            ft[l] = total.reshape(per * eight, LANES)
+            send, keep, line, lanes = leave(p)
+            for r in range(eight):
+                v = ft[l, pl.ds(r, per, stride=eight)] * gains[line]
+                fin[r, line, lanes : lanes + LANES] = v.astype(jnp.bfloat16)
+            send.start()
+            keep.start()
+
+    def moment(stage, n=0):
+        peer = (core_peer, x_peer, y_peer)[stage] if stage < 3 else device(dz=lax.rem(z + n, planes))
+        slot = stage + max(n - 1, 0)
+        return pltpu.make_async_remote_copy(
+            src_ref=sums.at[stage], dst_ref=pin.at[slot],
+            send_sem=ms.at[slot], recv_sem=mr.at[slot],
+            device_id=peer, device_id_type=MESH,
+        )
+
+    def moments(stage):
+        if stage == 0:
+            total = jnp.sum(jnp.sum(squares[...], axis=1), axis=1, keepdims=True)
+            count = jnp.sum(count_of(live), axis=1, keepdims=True)
+            lane = lax.broadcasted_iota(jnp.int32, (angles, LANES), 1)
+            both = jnp.where(lane == 0, total, jnp.where(lane == 1, count, 0.0))
+            both = jnp.concatenate([both, jnp.zeros((LANES - angles, LANES), jnp.float32)], axis=0)
+            sums[0] = both.T[:eight]
+            moment(0).start()
+        elif stage < 4:
+            moment(stage - 1).wait_recv()
+            sums[stage] = sums[stage - 1] + pin[stage - 1]
+            if stage < 3:
+                moment(stage).start()
+            else:
+                for n in range(1, planes):
+                    moment(3, n).start()
+        else:
+            total = sums[3]
+            for n in range(1, planes):
+                moment(3, n).wait_recv()
+                total += pin[3 + n - 1]
+            gain = lax.rsqrt(total[0:1] / (depth * total[1:2]) + 1e-06)
+            gains[...] = jnp.broadcast_to(gain, (LANES, LANES)).T[:angles]
+
+    def compute(phase):
+        d, h = phase // halves, phase % halves
+        if h == 0:
+            own_in[d].wait()
+        slant(d, h, 0)
+        if phase == 0:
+            meta.wait_recv()
+            cuts[1] = theirs[eight : eight + blocks]
+            k_rows = jnp.full((eight, onehot_lanes - LANES), -1, jnp.int32)
+            a_row = jnp.concatenate([jnp.broadcast_to(mine[0:1], (eight, LANES)), k_rows], axis=1)
+            b_row = jnp.concatenate([jnp.broadcast_to(theirs[0:1], (eight, LANES)), k_rows], axis=1)
+            b_row = pltpu.roll(b_row, blocks, 1)
+            lane = lax.broadcasted_iota(jnp.int32, a_row.shape, 1)
+            row = jnp.where(lane < blocks, a_row, b_row)
+            mask = y * (img_dev * grp) + g * img_dev
+            row = lax.bitwise_xor(row, jnp.full(row.shape, 0, jnp.int32) + mask)
+            number = lax.broadcasted_iota(jnp.int32, (images, onehot_lanes), 0)
+            hit = jnp.where(number == row[0:1], 1.0, 0.0).astype(jnp.bfloat16)
+            onehot[...] = hit[:, : 2 * blocks]
+        if h == 0:
+            core_in[d].wait_recv()
+        slant(d, h, 1)
+        for k in range(units):
+            cu = phase * units + k
+            stack(cu)
+            start_first(cu)
+
+    onehot_lanes = round_up(2 * blocks, LANES)
+
+    def count_of(ref):
+        return ref[...].astype(jnp.float32)
+
+    cus = depths * halves * units
+    for _, action in sorted(schedule(planes, kinds, depths * halves, units), key=lambda e: e[0]):
+        name, args = action[0], action[1:]
+        {
+            "compute": compute, "first": first, "second": second, "tick": tick,
+            "third": third, "finish": finish, "moments": moments,
+        }[name](*args)
+
+    meta.wait_send()
+    for copy in core_in:
+        copy.wait_send()
+    for cu in range(cus):
+        for l in range(2):
+            p = 2 * cu + l
+            n = 1 if late(p) else 2
+            for t in range(planes):
+                s1(p, t).wait_send()
+            for t in range(planes if late(p) else 1):
+                across(p, t, rx1.at[p, t, 1]).wait_send()
+            for way in range(2):
+                here = z if way == 0 else planes - 1 - z
+                for s in range(planes - 1):
+                    @pl.when(here < planes - 1 - s)
+                    def _(p=p, way=way, s=s, n=n):
+                        hop(p, way, s, held.at[p, way, s, pl.ds(0, n)]).wait_send()
+            send, keep, _, _ = leave(p)
+            keep.wait()
+            send.wait()
+    for stage in range(3):
+        moment(stage).wait_send()
+    for n in range(1, planes):
+        moment(3, n).wait_send()
+
+
+def far_first(planes):
+    order = []
+    for i in range(planes):
+        order.append(planes - 1 - i // 2 if i % 2 == 0 else i // 2)
+    return order
+
+
+def schedule(planes, kinds, phases, units):
+    events = []
+    step = 3.2
+    for phase in range(phases):
+        events.append((4.0 + step * phase, ("compute", phase)))
+    ready = 4.0 + step * phases
+    for stage in range(5):
+        events.append((ready + 6.0 * stage, ("moments", stage)))
+    gain = ready + 25.0
+    now = 7.0
+    for cu, kind in enumerate(kinds):
+        now += 6.0
+        at = now
+        events.append((at, ("first", cu)))
+        if kind == "vz":
+            now += 2.5
+            at += 6.0
+            events.append((at, ("second", cu)))
+        hop = 5.0 if kind == "zv" else 3.5
+        for tau in range(1, planes):
+            at += hop
+            events.append((at, ("tick", cu, tau)))
+        if kind == "zv":
+            at += 0.1
+            events.append((at, ("third", cu)))
+            at += 4.0
+        events.append((max(at + 0.2, gain), ("finish", cu)))
+    return events
+
+
+def fused(shapes, offsets, slant_weights, live, block_tile, image_slot):
+    planes, grp, scratch, kinds = shapes
+    blocks = block_tile.shape[0]
+    hs, depth = offsets.shape[1:]
+    angles = slant_weights.shape[0]
+    any_space = pl.BlockSpec(memory_space=pl.ANY)
+    vmem = pl.BlockSpec(memory_space=pltpu.VMEM)
+    return pl.pallas_call(
+        functools.partial(fused_kernel, (planes, grp, kinds)),
+        out_shape=jax.ShapeDtypeStruct((IMG_DEV, 2 * angles, depth), jnp.bfloat16),
+        in_specs=[any_space, vmem, vmem, vmem, vmem],
+        out_specs=any_space,
+        scratch_shapes=scratch,
+        compiler_params=pltpu.CompilerParams(
+            collective_id=2, has_side_effects=True, vmem_limit_bytes=VMEM_LIMIT
+        ),
+        name="calibrated_stack",
+    )(
+        offsets.reshape(blocks, 2, hs, depth),
+        live.T,
+        block_tile.reshape(1, blocks),
+        image_slot.reshape(1, blocks),
+        slant_weights.T,
+    )
+
+
+def buffers(planes, blocks, hs, depth, angles, images):
+    wide = 2 * LANES
+    per = 16
+    half = 2 * per
+    cus = (depth // wide) * (angles // per)
+    pieces, pairs = 2 * cus, per // 2
+    rows = 2 * 8
+    tile = (pairs, rows, LANES)
+    dma = pltpu.SemaphoreType.DMA
+    bf, f32, i32 = jnp.bfloat16, jnp.float32, jnp.int32
+    memory = [
+        ((2, blocks, hs, depth), bf),
+        ((angles * 8, 8 * hs), bf),
+        ((images, 2 * blocks), bf),
+        ((8 + blocks, LANES), i32),
+        ((8 + blocks, LANES), i32),
+        ((2, blocks, LANES), i32),
+        ((angles, 8, LANES), f32),
+        ((half, 2 * blocks, wide), bf),
+        ((pieces, planes, 2) + tile, f32),
+        ((pieces, planes, 2) + tile, bf),
+        ((pieces, planes, 2) + tile, bf),
+        ((pieces, planes) + tile, bf),
+        ((pieces, 2, planes - 1, 2) + tile, bf),
+        ((2, per * 8, LANES), f32),
+        ((2 * IMG_DEV, angles, depth), bf),
+        ((8, LANES), f32),
+        ((4, 8, LANES), f32),
+        ((3 + planes - 1, 8, LANES), f32),
+        ((angles, LANES), f32),
+    ]
+    size = sum(math.prod(s) * jnp.dtype(d).itemsize for s, d in memory)
+    scratch = [pltpu.VMEM(s, d) for s, d in memory]
+    depths = depth // wide
+    scratch += [
+        dma((depths,)), dma((depths,)), dma((depths,)), dma((1,)), dma((1,)),
+        dma((pieces, planes)), dma((pieces, planes)),
+        dma((pieces, planes)), dma((pieces, planes)),
+        dma((pieces, 2, planes - 1)), dma((pieces, 2, planes - 1)),
+        dma((pieces,)), dma((pieces,)), dma((pieces,)),
+        dma((3 + planes - 1,)), dma((3 + planes - 1,)),
+    ]
+    zfirst = (5 * cus + 4) // 8
+    kinds = ("zv",) * zfirst + ("vz",) * (cus - zfirst)
+    return size, scratch, kinds
+
+
+def local(offsets, slant_weights, live, block_tile, image_slot):
+    shots, grp = lax.axis_size("shot"), lax.axis_size("grp")
+    planes = shots // PAIR
+    blocks = block_tile.shape[0]
+    hs, depth = offsets.shape[1:]
+    angles = slant_weights.shape[0]
+    images = shots * IMG_DEV * grp
+    size, scratch, kinds = buffers(planes, blocks, hs, depth, angles, images)
+    args = (offsets, slant_weights, live, block_tile, image_slot)
+    if grp == 4 and size + (2 << 20) <= VMEM_LIMIT:
+        return fused((planes, grp, scratch, kinds), *args)
+    return staged(*args)
+
+
 def solution(mesh):
     placed = (
         P(("shot", "grp"), None, None),

time: 134 us -> 111 us (0.83)
  the two profiles are of different devices: /device:TPU:9 before, /device:TPU:0 now
where the time goes in v1:
time: 111 us
  Pallas kernels  109 us (98%)
  local copies, waits for them, and re-layouts  1.87 us (2%)
    pallas_call x1, Pallas kernels, fused(): pl.pallas_call(functools.partial(fused_kernel, (planes, grp, kinds)), out...  109 us

profile of v1, /device:TPU:0, one launch (start us, length us, event | category | flops | bytes accessed | tf_op | source)
XLA Modules:
  0.0 111.2 jit_solution(14443989791683322707)
XLA Ops:
  0.0 109.3 %calibrated_stack.1 = bf16[4,128,512]{2,1,0:T(8,128)(2,1)} custom-call(bf16[96,2,32,512]{3,2,1,0:T(8,128)(2,1)} %bitcast.5, s32[64,192]{1,0:T(8,128)} %bitcast.6, s32[1,96]{1,0:T(1,128)} %bitcast.8, s32[1,96]{1,0:T(1,128)} %bitcast.9, bf16[32,64]{1,0:T(8,128)(2,1)} %bitcast.7), custom_call_target="tpu_custom_call" | custom-call | tf_op jit(solution)/shard_map/calibrated_stack/pallas_call | solution.py:843
  109.3 1.9 %copy.7 = bf16[4,128,512]{2,1,0:T(8,128)(2,1)} copy(bf16[4,128,512]{2,1,0:T(8,128)(2,1)} %calibrated_stack.1) | data formatting | bytes 1048576

commit v2 on v0

--- a/solution.py
+++ b/solution.py
@@ -1,4 +1,5 @@
 import functools
+import math
 
 import jax
 import jax.numpy as jnp
@@ -12,6 +13,13 @@
 LANES = 128
 UNROLL = 8
 MESH = pl.DeviceIdType.MESH
+VMEM_LIMIT = 62 * 1024 * 1024
+SLANT_UNROLL = 2
+STACK_UNROLL = 4
+SCHEDULE = {
+    "compute": 3.2, "first": {"zv": 6.5, "vz": 10.5}, "begin": 0.2, "start": 12.7, "sub": 2.0,
+    "second": 11.4, "hop": {"zv": 15.9, "vz": 11.4}, "third": 0.3, "finish": 21.0, "moments": 2.5,
+}
 
 
 def place(grp):
@@ -317,7 +325,7 @@
                 finish(up, s, h)
 
 
-def local(offsets, slant_weights, live, block_tile, image_slot):
+def staged(offsets, slant_weights, live, block_tile, image_slot):
     shots, grp = lax.axis_size("shot"), lax.axis_size("grp")
     planes, size = shots // PAIR, PAIR * grp
     blocks = block_tile.shape[0]
@@ -403,6 +411,545 @@
     )(part, mom)
 
 
+def round_up(value, unit):
+    return -(-value // unit) * unit
+
+
+def fused_kernel(
+    shape, off, live_in, tile_in, slot_in, w_in, out,
+    live, tile, slot, weights, raw, wb, onehot, mine, theirs, cuts, squares, sl,
+    own, part, rx1, rxv, held, ft, fin, sums, pin, gains,
+    load_sem, in_sem, core_s, core_r, meta_s, meta_r, s1s, s1r, vs, vr, zs, zr, fs, fr, fl, ms, mr,
+):
+    planes, grp, kinds = shape
+    shot, g = lax.axis_index("shot"), lax.axis_index("grp")
+    z, y = lax.div(shot, PAIR), lax.rem(shot, PAIR)
+    x, c = lax.div(g, 2), lax.rem(g, 2)
+    blocks, hs, depth = raw.shape[1:]
+    angles = live.shape[0]
+    images = onehot.shape[0]
+    img_dev = out.shape[0]
+    per, wide = sl.shape[1], sl.shape[3]
+    pairs = per // 2
+    depths, groups = depth // wide, angles // per
+    cus = depths * groups
+    early = 2 * kinds.count("zv")
+    late_count = 2 * cus - early
+
+    def device(step=0, fy=False, fx=False, fc=False):
+        yy = 1 - y if fy else y
+        xx = 1 - x if fx else x
+        cc = 1 - c if fc else c
+        return ((z + step) * PAIR + yy, xx * 2 + cc)
+
+    core_peer, x_peer, y_peer = device(fc=True), device(fx=True), device(fy=True)
+    first_peer = (x_peer, y_peer)
+    second_peer = (y_peer, x_peer)
+
+    def remote(src, dst, send_sem, recv_sem, peer):
+        return pltpu.make_async_remote_copy(
+            src_ref=src, dst_ref=dst, send_sem=send_sem, recv_sem=recv_sem,
+            device_id=peer, device_id_type=MESH,
+        )
+
+    barrier = pltpu.get_barrier_semaphore()
+
+    def greet(peer):
+        pl.semaphore_signal(barrier, inc=1, device_id=peer, device_id_type=MESH)
+
+    for peer in (core_peer, x_peer, y_peer):
+        greet(peer)
+
+    @pl.when(z > 0)
+    def _():
+        greet(device(step=-1))
+
+    @pl.when(z < planes - 1)
+    def _():
+        greet(device(step=1))
+
+    loads = [
+        pltpu.make_async_copy(src, dst, load_sem.at[n])
+        for n, (src, dst) in enumerate(
+            ((w_in, weights), (live_in, live), (tile_in, tile), (slot_in, slot))
+        )
+    ]
+    for copy in loads:
+        copy.start()
+    own_in = [
+        pltpu.make_async_copy(
+            off.at[:, c, :, pl.ds(d * wide, wide)],
+            raw.at[0, :, :, pl.ds(d * wide, wide)],
+            in_sem.at[d],
+        )
+        for d in range(depths)
+    ]
+    for copy in own_in:
+        copy.start()
+    core_in = [
+        remote(
+            off.at[:, 1 - c, :, pl.ds(d * wide, wide)],
+            raw.at[1, :, :, pl.ds(d * wide, wide)],
+            core_s.at[d], core_r.at[d], core_peer,
+        )
+        for d in range(depths)
+    ]
+    meta = remote(mine, theirs, meta_s.at[0], meta_r.at[0], core_peer)
+
+    eight = 8
+    for copy in loads:
+        copy.wait()
+    ones = jnp.ones((angles, LANES), jnp.bfloat16)
+    spot = lax.broadcasted_iota(jnp.int32, (blocks, 2 * blocks), 1)
+    block = lax.broadcasted_iota(jnp.int32, (blocks, 2 * blocks), 0)
+
+    def cutoff(j):
+        pick = jnp.where(spot == 2 * block + j, 1.0, 0.0).astype(jnp.bfloat16)
+        flags = lax.dot_general(
+            pick, live[...].astype(jnp.float32).astype(jnp.bfloat16),
+            (((1,), (1,)), ((), ())), preferred_element_type=jnp.float32,
+        )
+        total = jnp.dot(flags.astype(jnp.bfloat16), ones, preferred_element_type=jnp.float32)
+        return total.astype(jnp.int32)
+
+    mine[0:eight] = jnp.full((eight, LANES), -1, jnp.int32)
+    mine[0:1, 0:blocks] = tile[...] * (img_dev * grp) + slot[...]
+    mine[eight : eight + blocks] = cutoff(1 - c)
+    cuts[0] = cutoff(c)
+
+    ends = jnp.where(z == 0, 1, 0) + jnp.where(z == planes - 1, 1, 0)
+    pl.semaphore_wait(barrier, 5 - ends)
+    core_in[0].start()
+    meta.start()
+    for copy in core_in[1:]:
+        copy.start()
+
+    rows = angles * eight
+    spread = lax.broadcasted_iota(jnp.int32, (rows, angles), 0)
+    which = lax.broadcasted_iota(jnp.int32, (rows, angles), 1)
+    pick = jnp.where(lax.div(spread, eight) == which, 1.0, 0.0).astype(jnp.bfloat16)
+    tall = lax.dot_general(
+        pick, weights[...], (((1,), (1,)), ((), ())), preferred_element_type=jnp.float32
+    ).astype(jnp.bfloat16)
+    line = lax.broadcasted_iota(jnp.int32, (hs, eight * hs), 0)
+    column = lax.broadcasted_iota(jnp.int32, (hs, eight * hs), 1)
+    copies = jnp.where(lax.rem(column, hs) == line, 1.0, 0.0).astype(jnp.bfloat16)
+    full = jnp.dot(tall, copies, preferred_element_type=jnp.float32)
+    line = lax.broadcasted_iota(jnp.int32, full.shape, 0)
+    column = lax.broadcasted_iota(jnp.int32, full.shape, 1)
+    wb[...] = jnp.where(lax.rem(line, eight) == lax.div(column, hs), full, 0.0).astype(jnp.bfloat16)
+    squares[...] = jnp.zeros_like(squares)
+
+    def slant(cu, r):
+        d, a0 = cu // groups, cu % groups * per
+        if r == 0 and cu % groups == 0:
+            own_in[d].wait()
+        if r == 1 and cu == 0:
+            meta.wait_recv()
+            cuts[1] = theirs[eight : eight + blocks]
+            select_rows()
+        if r == 1 and cu % groups == 0:
+            core_in[d].wait_recv()
+
+        def body(i, _):
+            lhs = wb[a0 * eight : (a0 + per) * eight]
+            lanes = slice(d * wide, (d + 1) * wide)
+            a = lax.broadcasted_iota(jnp.int32, (per, 2 * eight, LANES), 0) + a0
+            total = squares[a0 : a0 + per]
+            for n in range(SLANT_UNROLL):
+                start = (i * SLANT_UNROLL + n) * 2 * eight
+                alive = cuts[r, pl.ds(start, 2 * eight)][None] > a
+                ys = []
+                for k in range(2):
+                    data = raw[r, pl.ds(start + k * eight, eight), :, lanes]
+                    data = data.reshape(eight * hs, wide)
+                    y = jnp.dot(lhs, data, preferred_element_type=jnp.float32)
+                    ys.append(y.reshape(per, eight, wide))
+                for k in range(wide // LANES):
+                    cut = slice(k * LANES, (k + 1) * LANES)
+                    v = jnp.concatenate([ys[0][:, :, cut], ys[1][:, :, cut]], axis=1)
+                    v = jnp.where(alive, v, 0.0)
+                    q = v * v
+                    total += q[:, :eight] + q[:, eight:]
+                    sl[cu % 2, :, pl.ds(r * blocks + start, 2 * eight), cut] = v.astype(jnp.bfloat16)
+            squares[a0 : a0 + per] = total
+            return 0
+
+        lax.fori_loop(0, blocks // (2 * eight * SLANT_UNROLL), body, 0)
+
+    def select_rows():
+        lanes = round_up(2 * blocks, LANES)
+        rest = jnp.full((eight, lanes - LANES), -1, jnp.int32)
+        a_row = jnp.concatenate([jnp.broadcast_to(mine[0:1], (eight, LANES)), rest], axis=1)
+        b_row = jnp.concatenate([jnp.broadcast_to(theirs[0:1], (eight, LANES)), rest], axis=1)
+        b_row = pltpu.roll(b_row, blocks, 1)
+        lane = lax.broadcasted_iota(jnp.int32, a_row.shape, 1)
+        row = jnp.where(lane < blocks, a_row, b_row)
+        mask = y * (img_dev * grp) + g * img_dev
+        row = lax.bitwise_xor(row, jnp.full(row.shape, 0, jnp.int32) + mask)
+        number = lax.broadcasted_iota(jnp.int32, (images, lanes), 0)
+        hit = jnp.where(number == row[0:1], 1.0, 0.0).astype(jnp.bfloat16)
+        onehot[...] = hit[:, : 2 * blocks]
+
+    def stack(cu):
+        def body(i, _):
+            for n in range(STACK_UNROLL):
+                m = i * STACK_UNROLL + n
+                ys = [
+                    jnp.dot(onehot[...], sl[cu % 2, 2 * m + k], preferred_element_type=jnp.float32)
+                    for k in range(2)
+                ]
+                for l in range(2):
+                    p = 2 * cu + l
+                    cut = slice(l * LANES, (l + 1) * LANES)
+                    for t in range(planes):
+                        for ry in range(2):
+                            for rx in range(2):
+                                r = ((t * 2 + ry) * 2 + rx) * eight
+                                v = [ys[k][r : r + eight, cut] for k in range(2)]
+                                v = jnp.concatenate(v, axis=0)
+                                one, two = (rx, ry) if l == 0 else (ry, rx)
+                                if one == 0:
+                                    own[p, t, two, m] = v
+                                else:
+                                    part[p, t, two, m] = v.astype(jnp.bfloat16)
+            return 0
+
+        lax.fori_loop(0, pairs // STACK_UNROLL, body, 0)
+
+    def late(cu):
+        return kinds[cu] == "vz"
+
+    def s1(cu, l, t):
+        p = 2 * cu + l
+        return remote(part.at[p, t], rx1.at[p, t], s1s.at[0], s1r.at[cu, t], first_peer[l])
+
+    def across_slot(cu, t):
+        return early // 2 + (cu - early // 2) * planes + t if late(cu) else cu
+
+    def across(cu, l, t, source):
+        p, slot = 2 * cu + l, across_slot(cu, t)
+        kind = 1 if late(cu) else 0
+        return remote(source, rxv.at[p, t], vs.at[kind], vr.at[slot], second_peer[l])
+
+    def arrived(region, sem):
+        remote(region, region, ms.at[0], sem, core_peer).wait_recv()
+
+    def hop(cu, way, s, source):
+        p, n = pl.ds(2 * cu, 2), pl.ds(0, 1 if late(cu) else 2)
+        kind = 1 if late(cu) else 0
+        return remote(
+            source, held.at[p, way, s, n], zs.at[kind, way, s], zr.at[cu, way, s],
+            device(step=1 - 2 * way),
+        )
+
+    def begin(cu, t):
+        source = rx1.at[pl.ds(2 * cu, 2), t, pl.ds(0, 1 if late(cu) else 2)]
+        if t > 0:
+            @pl.when(z == 0)
+            def _():
+                hop(cu, 0, planes - 1 - t, source).start()
+        if t < planes - 1:
+            @pl.when(z == planes - 1)
+            def _():
+                hop(cu, 1, t, source).start()
+
+    def start(cu):
+        for t in far_first(planes):
+            for l in range(2):
+                s1(cu, l, t).start()
+
+    def first(cu, t):
+        arrived(rx1.at[pl.ds(2 * cu, 2), t], s1r.at[cu, t])
+        for l in range(2):
+            p = 2 * cu + l
+            for k in (1, 0):
+                total = own[p, t, k] + rx1[p, t, k].astype(jnp.float32)
+                own[p, t, k] = total
+                rx1[p, t, k] = total.astype(jnp.bfloat16)
+            if late(cu):
+                across(cu, l, t, rx1.at[p, t, 1]).start()
+        if not late(cu):
+            begin(cu, t)
+
+    def second(cu, t):
+        arrived(rxv.at[pl.ds(2 * cu, 2), t], vr.at[across_slot(cu, t)])
+        for l in range(2):
+            p = 2 * cu + l
+            total = own[p, t, 0] + rxv[p, t].astype(jnp.float32)
+            own[p, t, 0] = total
+            rx1[p, t, 0] = total.astype(jnp.bfloat16)
+        begin(cu, t)
+
+    def tick(cu, tau, way):
+        here = z if way == 0 else planes - 1 - z
+        s = tau - here
+        target = planes - 1 - s if way == 0 else s
+        n = 1 if late(cu) else 2
+
+        @pl.when((here >= 1) & (s >= 0))
+        def _():
+            message = held.at[pl.ds(2 * cu, 2), way, s, pl.ds(0, n)]
+            hop(cu, way, s, message).wait_recv()
+            for l in range(2):
+                p = 2 * cu + l
+                for k in range(n):
+                    value = held[p, way, s, k].astype(jnp.float32) + own[p, target, k]
+                    if tau < planes - 1:
+                        held[p, way, s, k] = value.astype(jnp.bfloat16)
+                    else:
+                        own[p, target, k] = value
+            if tau < planes - 1:
+                hop(cu, way, s, message).start()
+
+    def third(cu):
+        for l in range(2):
+            p = 2 * cu + l
+            rx1[p, z, 1] = own[p, z, 1].astype(jnp.bfloat16)
+            across(cu, l, 0, rx1.at[p, z, 1]).start()
+
+    def leave(line, lanes):
+        row = pl.multiple_of(c * angles + line.start, per)
+        view = out.at[:, pl.ds(row, line.size), pl.ds(lanes.start, lanes.size)]
+        send = remote(fin.at[pl.ds(img_dev, img_dev), line, lanes], view, fs.at[0], fr.at[0], core_peer)
+        keep = pltpu.make_async_copy(fin.at[pl.ds(0, img_dev), line, lanes], view, fl.at[0])
+        return send, keep
+
+    def finish(cu):
+        if not late(cu):
+            arrived(rxv.at[pl.ds(2 * cu, 2), 0], vr.at[across_slot(cu, 0)])
+        a0, lane0 = cu % groups * per, cu // groups * wide
+        for l in range(2):
+            p = 2 * cu + l
+            total = own[p, z, 0]
+            if not late(cu):
+                total += rxv[p, 0].astype(jnp.float32)
+            ft[l] = total.reshape(per * eight, LANES)
+            lanes = slice(lane0 + l * LANES, lane0 + (l + 1) * LANES)
+            for r in range(eight):
+                v = ft[l, pl.ds(r, per, stride=eight)] * gains[a0 : a0 + per]
+                fin[r, a0 : a0 + per, lanes] = v.astype(jnp.bfloat16)
+        for copy in leave(pl.ds(a0, per), pl.ds(lane0, wide)):
+            copy.start()
+
+    def moment(stage):
+        peer = (core_peer, x_peer, y_peer)[stage]
+        return remote(sums.at[stage], pin.at[stage], ms.at[stage], mr.at[stage], peer)
+
+    def passing(way):
+        n = 3 + way
+        return remote(sums.at[n + 1], pin.at[n], ms.at[n], mr.at[n], device(step=1 - 2 * way))
+
+    def moments(stage):
+        if stage == 0:
+            total = jnp.sum(jnp.sum(squares[...], axis=1), axis=1, keepdims=True)
+            count = jnp.sum(live[...].astype(jnp.float32), axis=1, keepdims=True)
+            lane = lax.broadcasted_iota(jnp.int32, (angles, LANES), 1)
+            both = jnp.where(lane == 0, total, jnp.where(lane == 1, count, 0.0))
+            both = jnp.concatenate([both, jnp.zeros((LANES - angles, LANES), jnp.float32)], axis=0)
+            sums[0] = both.T[:eight]
+            moment(0).start()
+            return
+        if stage <= 3:
+            moment(stage - 1).wait_recv()
+            sums[stage] = sums[stage - 1] + pin[stage - 1]
+            if stage < 3:
+                moment(stage).start()
+                return
+            sums[6] = sums[3]
+        tau = stage - 3
+        if tau < planes:
+            for way in range(2):
+                here = z if way == 0 else planes - 1 - z
+
+                @pl.when(here == tau)
+                def _(way=way):
+                    if tau > 0:
+                        passing(way).wait_recv()
+                        sums[6] = sums[6] + pin[3 + way]
+                        sums[4 + way] = sums[3] + pin[3 + way]
+                    else:
+                        sums[4 + way] = sums[3]
+                    if tau < planes - 1:
+                        passing(way).start()
+        else:
+            total = sums[6]
+            gain = lax.rsqrt(total[0:1] / (depth * total[1:2]) + 1e-06)
+            gains[...] = jnp.broadcast_to(gain, (LANES, LANES)).T[:angles]
+
+    run = {
+        "slant": slant, "stack": stack, "start": start, "first": first, "second": second,
+        "tick": tick, "third": third, "finish": finish, "moments": moments,
+    }
+    for _, action in sorted(schedule(planes, kinds), key=lambda e: e[0]):
+        run[action[0]](*action[1:])
+
+    meta.wait_send()
+    for copy in core_in:
+        copy.wait_send()
+    remote(part, rx1, s1s.at[0], s1r.at[0, 0], core_peer).wait_send()
+    if early:
+        region = rxv.at[pl.ds(0, early), 0]
+        remote(region, region, vs.at[0], vr.at[0], core_peer).wait_send()
+    if late_count:
+        region = rxv.at[pl.ds(early, late_count)]
+        remote(region, region, vs.at[1], vr.at[0], core_peer).wait_send()
+    for way in range(2):
+        here = z if way == 0 else planes - 1 - z
+
+        @pl.when(here < planes - 1)
+        def _(way=way):
+            passing(way).wait_send()
+
+        for s in range(planes - 1):
+            @pl.when(here < planes - 1 - s)
+            def _(way=way, s=s):
+                for kind, region in enumerate(
+                    (
+                        held.at[pl.ds(0, early), way, s],
+                        held.at[pl.ds(early, late_count), way, s, pl.ds(0, 1)],
+                    )
+                ):
+                    if (early, late_count)[kind]:
+                        remote(
+                            region, region, zs.at[kind, way, s], zr.at[0, way, s], core_peer
+                        ).wait_send()
+    for stage in range(3):
+        moment(stage).wait_send()
+    send, keep = leave(pl.ds(0, angles), pl.ds(0, depth))
+    keep.wait()
+    send.wait()
+
+
+def far_first(planes):
+    return [planes - 1 - i // 2 if i % 2 == 0 else i // 2 for i in range(planes)]
+
+
+def schedule(planes, kinds):
+    compute, spacing, lag, sub = SCHEDULE["compute"], SCHEDULE["first"], SCHEDULE["start"], SCHEDULE["sub"]
+    cus = len(kinds)
+    events = [(-2.0, ("slant", 0, 0)), (-1.0, ("slant", 1, 0))]
+    for cu in range(cus):
+        at = compute * cu
+        if cu > 1:
+            events.append((at, ("slant", cu, 0)))
+        events.append((at + 0.1 * compute, ("slant", cu, 1)))
+        events.append((at + 0.2 * compute, ("stack", cu)))
+    done = compute * cus
+    for stage in range(3 + planes + 1):
+        events.append((done + SCHEDULE["moments"] * stage, ("moments", stage)))
+    gain = done + SCHEDULE["moments"] * (3 + planes) + 0.1
+    now = SCHEDULE["begin"]
+    for cu, kind in enumerate(kinds):
+        at = now
+        events.append((max(compute * cu + 0.3 * compute, at - lag), ("start", cu)))
+        at = max(at, compute * cu + 0.3 * compute + 0.1)
+        for i, t in enumerate(far_first(planes)):
+            events.append((at + i * sub, ("first", cu, t)))
+        now += spacing[kind]
+        at += (planes - 1) * sub
+        if kind == "vz":
+            at += SCHEDULE["second"] - (planes - 1) * sub
+            for i, t in enumerate(far_first(planes)):
+                events.append((at + i * sub, ("second", cu, t)))
+            at += (planes - 1) * sub
+        for tau in range(1, planes):
+            at += SCHEDULE["hop"][kind]
+            for way in range(2):
+                events.append((at, ("tick", cu, tau, way)))
+        if kind == "zv":
+            at += SCHEDULE["third"]
+            events.append((at, ("third", cu)))
+            at += SCHEDULE["finish"]
+        events.append((max(at + 0.01, gain), ("finish", cu)))
+    return events
+
+
+def fused(shapes, offsets, slant_weights, live, block_tile, image_slot):
+    planes, grp, scratch, kinds = shapes
+    blocks = block_tile.shape[0]
+    hs, depth = offsets.shape[1:]
+    angles = slant_weights.shape[0]
+    any_space = pl.BlockSpec(memory_space=pl.ANY)
+    return pl.pallas_call(
+        functools.partial(fused_kernel, (planes, grp, kinds)),
+        out_shape=jax.ShapeDtypeStruct((IMG_DEV, 2 * angles, depth), jnp.bfloat16),
+        in_specs=[any_space] * 5,
+        out_specs=any_space,
+        scratch_shapes=scratch,
+        compiler_params=pltpu.CompilerParams(
+            collective_id=2, has_side_effects=True, vmem_limit_bytes=VMEM_LIMIT
+        ),
+        name="calibrated_stack",
+    )(
+        offsets.reshape(blocks, 2, hs, depth),
+        live.T,
+        block_tile.reshape(1, blocks),
+        image_slot.reshape(1, blocks),
+        slant_weights.T,
+    )
+
+
+def buffers(planes, blocks, hs, depth, angles, images):
+    wide, per = 2 * LANES, 16
+    cus = (depth // wide) * (angles // per)
+    pieces = 2 * cus
+    tile = (per // 2, 16, LANES)
+    dma = pltpu.SemaphoreType.DMA
+    bf, f32, i32 = jnp.bfloat16, jnp.float32, jnp.int32
+    early = (5 * cus + 4) // 8
+    kinds = ("zv",) * early + ("vz",) * (cus - early)
+    memory = [
+        ((angles, 2 * blocks), i32),
+        ((1, blocks), i32),
+        ((1, blocks), i32),
+        ((hs, angles), bf),
+        ((2, blocks, hs, depth), bf),
+        ((angles * 8, 8 * hs), bf),
+        ((images, 2 * blocks), bf),
+        ((8 + blocks, LANES), i32),
+        ((8 + blocks, LANES), i32),
+        ((2, blocks, LANES), i32),
+        ((angles, 8, LANES), f32),
+        ((2, per, 2 * blocks, wide), bf),
+        ((pieces, planes, 2) + tile, f32),
+        ((pieces, planes, 2) + tile, bf),
+        ((pieces, planes, 2) + tile, bf),
+        ((pieces, planes) + tile, bf),
+        ((pieces, 2, planes - 1, 2) + tile, bf),
+        ((2, per * 8, LANES), f32),
+        ((2 * IMG_DEV, angles, depth), bf),
+        ((7, 8, LANES), f32),
+        ((5, 8, LANES), f32),
+        ((angles, LANES), f32),
+    ]
+    size = sum(math.prod(s) * jnp.dtype(d).itemsize for s, d in memory)
+    scratch = [pltpu.VMEM(s, d) for s, d in memory]
+    depths = depth // wide
+    scratch += [
+        dma((4,)), dma((depths,)), dma((depths,)), dma((depths,)), dma((1,)), dma((1,)),
+        dma((1,)), dma((cus, planes)),
+        dma((2,)), dma((early + (cus - early) * planes,)),
+        dma((2, 2, planes - 1)), dma((cus, 2, planes - 1)),
+        dma((1,)), dma((1,)), dma((1,)), dma((5,)), dma((5,)),
+    ]
+    return size, scratch, kinds
+
+
+def local(offsets, slant_weights, live, block_tile, image_slot):
+    shots, grp = lax.axis_size("shot"), lax.axis_size("grp")
+    planes = shots // PAIR
+    blocks = block_tile.shape[0]
+    hs, depth = offsets.shape[1:]
+    angles = slant_weights.shape[0]
+    images = shots * IMG_DEV * grp
+    size, scratch, kinds = buffers(planes, blocks, hs, depth, angles, images)
+    args = (offsets, slant_weights, live, block_tile, image_slot)
+    if grp == 4 and size + (2 << 20) <= VMEM_LIMIT:
+        return fused((planes, grp, scratch, kinds), *args)
+    return staged(*args)
+
+
 def solution(mesh):
     placed = (
         P(("shot", "grp"), None, None),

time: 134 us -> 96.6 us (0.72)
  the two profiles are of different devices: /device:TPU:9 before, /device:TPU:0 now
where the time goes in v2:
time: 96.6 us; the launch traced here: 96.4 us
  Pallas kernels  94.5 us (98%)
  local copies, waits for them, and re-layouts  1.87 us (2%)
    pallas_call x1, Pallas kernels, fused(): pl.pallas_call(functools.partial(fused_kernel, (planes, grp, kinds)), out...  94.5 us

profile of v2, /device:TPU:0, one launch (start us, length us, event | category | flops | bytes accessed | tf_op | source)
XLA Modules:
  0.0 96.4 jit_solution(390503337644184402)
XLA Ops:
  0.0 94.5 %calibrated_stack.1 = bf16[4,128,512]{2,1,0:T(8,128)(2,1)} custom-call(bf16[96,2,32,512]{3,2,1,0:T(8,128)(2,1)} %bitcast.5, s32[64,192]{1,0:T(8,128)} %bitcast.6, s32[1,96]{1,0:T(1,128)} %bitcast.8, s32[1,96]{1,0:T(1,128)} %bitcast.9, bf16[32,64]{1,0:T(8,128)(2,1)} %bitcast.7), custom_call_target="tpu_custom_call" | custom-call | tf_op jit(solution)/shard_map/calibrated_stack/pallas_call | solution.py:874
  94.5 1.9 %copy.7 = bf16[4,128,512]{2,1,0:T(8,128)(2,1)} copy(bf16[4,128,512]{2,1,0:T(8,128)(2,1)} %calibrated_stack.1) | data formatting | bytes 1048576

commit v3 on v2

--- a/solution.py
+++ b/solution.py
@@ -17,8 +17,9 @@
 SLANT_UNROLL = 2
 STACK_UNROLL = 4
 SCHEDULE = {
-    "compute": 3.2, "first": {"zv": 6.5, "vz": 10.5}, "begin": 0.2, "start": 12.7, "sub": 2.0,
-    "second": 11.4, "hop": {"zv": 15.9, "vz": 11.4}, "third": 0.3, "finish": 21.0, "moments": 2.5,
+    "compute": 3.19, "first": {"zv": 7.98, "vz": 14.69}, "begin": 3.59, "start": 15.93, "sub": 2.8,
+    "second": 19.16, "hop": {"zv": 14.36, "vz": 19.05}, "third": 32.32, "finish": 0.39,
+    "moments": 16.35,
 }
 
 

time: 96.6 us -> 80.8 us (0.84)
  Pallas kernels: 94.5 us -> 78.7 us
    pallas_call x1, Pallas kernels: 94.5 us -> 78.7 us  [fused(): pl.pallas_call(functools.partial(fused_kernel, (planes, grp, kinds)), out...]
where the time goes in v3:
time: 80.8 us; the launch traced here: 80.6 us
  Pallas kernels  78.7 us (97%)
  local copies, waits for them, and re-layouts  1.87 us (2%)
    pallas_call x1, Pallas kernels, fused(): pl.pallas_call(functools.partial(fused_kernel, (planes, grp, kinds)), out...  78.7 us
    unnamed x1, local copies, waits for them, and re-layouts  1.87 us

profile of v3, /device:TPU:0, one launch (start us, length us, event | category | flops | bytes accessed | tf_op | source)
XLA Modules:
  0.0 80.6 jit_solution(9467311311278933024)
XLA Ops:
  0.0 78.7 %calibrated_stack.1 = bf16[4,128,512]{2,1,0:T(8,128)(2,1)} custom-call(bf16[96,2,32,512]{3,2,1,0:T(8,128)(2,1)} %bitcast.5, s32[64,192]{1,0:T(8,128)} %bitcast.6, s32[1,96]{1,0:T(1,128)} %bitcast.8, s32[1,96]{1,0:T(1,128)} %bitcast.9, bf16[32,64]{1,0:T(8,128)(2,1)} %bitcast.7), custom_call_target="tpu_custom_call" | custom-call | tf_op jit(solution)/shard_map/calibrated_stack/pallas_call | solution.py:875
  78.7 1.9 %copy.7 = bf16[4,128,512]{2,1,0:T(8,128)(2,1)} copy(bf16[4,128,512]{2,1,0:T(8,128)(2,1)} %calibrated_stack.1) | data formatting | bytes 1048576

commit v4 on v3

--- a/solution.py
+++ b/solution.py
@@ -420,7 +420,7 @@
     shape, off, live_in, tile_in, slot_in, w_in, out,
     live, tile, slot, weights, raw, wb, onehot, mine, theirs, cuts, squares, sl,
     own, part, rx1, rxv, held, ft, fin, sums, pin, gains,
-    load_sem, in_sem, core_s, core_r, meta_s, meta_r, s1s, s1r, vs, vr, zs, zr, fs, fr, fl, ms, mr,
+    load_sem, in_sem, core_s, core_r, meta_s, meta_r, s1s, s1r, vs, vr, zs, zr, fs, fr, ms, mr,
 ):
     planes, grp, kinds = shape
     shot, g = lax.axis_index("shot"), lax.axis_index("grp")
@@ -487,13 +487,14 @@
     ]
     for copy in own_in:
         copy.start()
+    spans = [(0, LANES), (LANES, wide - LANES)] + [(d * wide, wide) for d in range(1, depths)]
     core_in = [
         remote(
-            off.at[:, 1 - c, :, pl.ds(d * wide, wide)],
-            raw.at[1, :, :, pl.ds(d * wide, wide)],
-            core_s.at[d], core_r.at[d], core_peer,
-        )
-        for d in range(depths)
+            off.at[:, 1 - c, :, pl.ds(lane, size)],
+            raw.at[1, :, :, pl.ds(lane, size)],
+            core_s.at[n], core_r.at[n], core_peer,
+        )
+        for n, (lane, size) in enumerate(spans)
     ]
     meta = remote(mine, theirs, meta_s.at[0], meta_r.at[0], core_peer)
 
@@ -541,20 +542,21 @@
     wb[...] = jnp.where(lax.rem(line, eight) == lax.div(column, hs), full, 0.0).astype(jnp.bfloat16)
     squares[...] = jnp.zeros_like(squares)
 
-    def slant(cu, r):
+    def slant(cu, r, tiles=(0, 1)):
         d, a0 = cu // groups, cu % groups * per
+        lane0, size = tiles[0] * LANES, len(tiles) * LANES
         if r == 0 and cu % groups == 0:
             own_in[d].wait()
-        if r == 1 and cu == 0:
+        if r == 1 and cu == 0 and lane0 == 0:
             meta.wait_recv()
             cuts[1] = theirs[eight : eight + blocks]
             select_rows()
         if r == 1 and cu % groups == 0:
-            core_in[d].wait_recv()
+            core_in[spans.index((d * wide + lane0, size))].wait_recv()
 
         def body(i, _):
             lhs = wb[a0 * eight : (a0 + per) * eight]
-            lanes = slice(d * wide, (d + 1) * wide)
+            lanes = slice(d * wide + lane0, d * wide + lane0 + size)
             a = lax.broadcasted_iota(jnp.int32, (per, 2 * eight, LANES), 0) + a0
             total = squares[a0 : a0 + per]
             for n in range(SLANT_UNROLL):
@@ -563,16 +565,17 @@
                 ys = []
                 for k in range(2):
                     data = raw[r, pl.ds(start + k * eight, eight), :, lanes]
-                    data = data.reshape(eight * hs, wide)
+                    data = data.reshape(eight * hs, size)
                     y = jnp.dot(lhs, data, preferred_element_type=jnp.float32)
-                    ys.append(y.reshape(per, eight, wide))
-                for k in range(wide // LANES):
+                    ys.append(y.reshape(per, eight, size))
+                for k in range(len(tiles)):
                     cut = slice(k * LANES, (k + 1) * LANES)
+                    to = slice(lane0 + k * LANES, lane0 + (k + 1) * LANES)
                     v = jnp.concatenate([ys[0][:, :, cut], ys[1][:, :, cut]], axis=1)
                     v = jnp.where(alive, v, 0.0)
                     q = v * v
                     total += q[:, :eight] + q[:, eight:]
-                    sl[cu % 2, :, pl.ds(r * blocks + start, 2 * eight), cut] = v.astype(jnp.bfloat16)
+                    sl[cu % 2, :, pl.ds(r * blocks + start, 2 * eight), to] = v.astype(jnp.bfloat16)
             squares[a0 : a0 + per] = total
             return 0
 
@@ -592,17 +595,19 @@
         hit = jnp.where(number == row[0:1], 1.0, 0.0).astype(jnp.bfloat16)
         onehot[...] = hit[:, : 2 * blocks]
 
-    def stack(cu):
+    def stack(cu, tiles=(0, 1)):
+        near = slice(tiles[0] * LANES, (tiles[-1] + 1) * LANES)
+
         def body(i, _):
-            for n in range(STACK_UNROLL):
-                m = i * STACK_UNROLL + n
+            for o in range(STACK_UNROLL):
+                m = i * STACK_UNROLL + o
                 ys = [
-                    jnp.dot(onehot[...], sl[cu % 2, 2 * m + k], preferred_element_type=jnp.float32)
+                    jnp.dot(onehot[...], sl[cu % 2, 2 * m + k, :, near], preferred_element_type=jnp.float32)
                     for k in range(2)
                 ]
-                for l in range(2):
+                for n, l in enumerate(tiles):
                     p = 2 * cu + l
-                    cut = slice(l * LANES, (l + 1) * LANES)
+                    cut = slice(n * LANES, (n + 1) * LANES)
                     for t in range(planes):
                         for ry in range(2):
                             for rx in range(2):
@@ -636,28 +641,34 @@
     def arrived(region, sem):
         remote(region, region, ms.at[0], sem, core_peer).wait_recv()
 
-    def hop(cu, way, s, source):
-        p, n = pl.ds(2 * cu, 2), pl.ds(0, 1 if late(cu) else 2)
+    def messages(cu):
+        return [(0,), (1,)] if late(cu) else [(0, 1)]
+
+    def hop(cu, tiles, way, s, source):
+        p, n = pl.ds(2 * cu + tiles[0], len(tiles)), pl.ds(0, 1 if late(cu) else 2)
         kind = 1 if late(cu) else 0
+        slot = early // 2 + 2 * (cu - early // 2) + tiles[0] if late(cu) else cu
         return remote(
-            source, held.at[p, way, s, n], zs.at[kind, way, s], zr.at[cu, way, s],
+            source, held.at[p, way, s, n], zs.at[kind, way, s], zr.at[slot, way, s],
             device(step=1 - 2 * way),
         )
 
     def begin(cu, t):
-        source = rx1.at[pl.ds(2 * cu, 2), t, pl.ds(0, 1 if late(cu) else 2)]
-        if t > 0:
-            @pl.when(z == 0)
-            def _():
-                hop(cu, 0, planes - 1 - t, source).start()
-        if t < planes - 1:
-            @pl.when(z == planes - 1)
-            def _():
-                hop(cu, 1, t, source).start()
-
-    def start(cu):
+        for tiles in messages(cu):
+            p = pl.ds(2 * cu + tiles[0], len(tiles))
+            source = rx1.at[p, t, pl.ds(0, 1 if late(cu) else 2)]
+            if t > 0:
+                @pl.when(z == 0)
+                def _(tiles=tiles, source=source):
+                    hop(cu, tiles, 0, planes - 1 - t, source).start()
+            if t < planes - 1:
+                @pl.when(z == planes - 1)
+                def _(tiles=tiles, source=source):
+                    hop(cu, tiles, 1, t, source).start()
+
+    def start(cu, tiles=(0, 1)):
         for t in far_first(planes):
-            for l in range(2):
+            for l in tiles:
                 s1(cu, l, t).start()
 
     def first(cu, t):
@@ -690,18 +701,20 @@
 
         @pl.when((here >= 1) & (s >= 0))
         def _():
-            message = held.at[pl.ds(2 * cu, 2), way, s, pl.ds(0, n)]
-            hop(cu, way, s, message).wait_recv()
-            for l in range(2):
-                p = 2 * cu + l
-                for k in range(n):
-                    value = held[p, way, s, k].astype(jnp.float32) + own[p, target, k]
-                    if tau < planes - 1:
-                        held[p, way, s, k] = value.astype(jnp.bfloat16)
-                    else:
-                        own[p, target, k] = value
-            if tau < planes - 1:
-                hop(cu, way, s, message).start()
+            for tiles in messages(cu):
+                p = pl.ds(2 * cu + tiles[0], len(tiles))
+                message = held.at[p, way, s, pl.ds(0, n)]
+                hop(cu, tiles, way, s, message).wait_recv()
+                for l in tiles:
+                    p = 2 * cu + l
+                    for k in range(n):
+                        value = held[p, way, s, k].astype(jnp.float32) + own[p, target, k]
+                        if tau < planes - 1:
+                            held[p, way, s, k] = value.astype(jnp.bfloat16)
+                        else:
+                            own[p, target, k] = value
+                if tau < planes - 1:
+                    hop(cu, tiles, way, s, message).start()
 
     def third(cu):
         for l in range(2):
@@ -712,9 +725,7 @@
     def leave(line, lanes):
         row = pl.multiple_of(c * angles + line.start, per)
         view = out.at[:, pl.ds(row, line.size), pl.ds(lanes.start, lanes.size)]
-        send = remote(fin.at[pl.ds(img_dev, img_dev), line, lanes], view, fs.at[0], fr.at[0], core_peer)
-        keep = pltpu.make_async_copy(fin.at[pl.ds(0, img_dev), line, lanes], view, fl.at[0])
-        return send, keep
+        return remote(fin.at[:, line, lanes], view, fs.at[0], fr.at[0], core_peer)
 
     def finish(cu):
         if not late(cu):
@@ -729,9 +740,12 @@
             lanes = slice(lane0 + l * LANES, lane0 + (l + 1) * LANES)
             for r in range(eight):
                 v = ft[l, pl.ds(r, per, stride=eight)] * gains[a0 : a0 + per]
-                fin[r, a0 : a0 + per, lanes] = v.astype(jnp.bfloat16)
-        for copy in leave(pl.ds(a0, per), pl.ds(lane0, wide)):
-            copy.start()
+                if r < img_dev:
+                    row = pl.multiple_of(c * angles + a0, per)
+                    out[r, pl.ds(row, per), lanes] = v.astype(jnp.bfloat16)
+                else:
+                    fin[r - img_dev, a0 : a0 + per, lanes] = v.astype(jnp.bfloat16)
+        leave(pl.ds(a0, per), pl.ds(lane0, wide)).start()
 
     def moment(stage):
         peer = (core_peer, x_peer, y_peer)[stage]
@@ -817,9 +831,7 @@
                         ).wait_send()
     for stage in range(3):
         moment(stage).wait_send()
-    send, keep = leave(pl.ds(0, angles), pl.ds(0, depth))
-    keep.wait()
-    send.wait()
+    leave(pl.ds(0, angles), pl.ds(0, depth)).wait()
 
 
 def far_first(planes):
@@ -829,8 +841,12 @@
 def schedule(planes, kinds):
     compute, spacing, lag, sub = SCHEDULE["compute"], SCHEDULE["first"], SCHEDULE["start"], SCHEDULE["sub"]
     cus = len(kinds)
-    events = [(-2.0, ("slant", 0, 0)), (-1.0, ("slant", 1, 0))]
-    for cu in range(cus):
+    events = [(-2.0, ("slant", 0, 0))]
+    for l in range(2):
+        for n, name in enumerate((("slant", 0, 1), ("stack", 0), ("start", 0))):
+            events.append((-1.0 + 0.1 * n + 0.4 * l, name + ((l,),)))
+    events.append((-0.3, ("slant", 1, 0)))
+    for cu in range(1, cus):
         at = compute * cu
         if cu > 1:
             events.append((at, ("slant", cu, 0)))
@@ -843,7 +859,8 @@
     now = SCHEDULE["begin"]
     for cu, kind in enumerate(kinds):
         at = now
-        events.append((max(compute * cu + 0.3 * compute, at - lag), ("start", cu)))
+        if cu > 0:
+            events.append((max(compute * cu + 0.3 * compute, at - lag), ("start", cu)))
         at = max(at, compute * cu + 0.3 * compute + 0.1)
         for i, t in enumerate(far_first(planes)):
             events.append((at + i * sub, ("first", cu, t)))
@@ -874,9 +891,9 @@
     any_space = pl.BlockSpec(memory_space=pl.ANY)
     return pl.pallas_call(
         functools.partial(fused_kernel, (planes, grp, kinds)),
-        out_shape=jax.ShapeDtypeStruct((IMG_DEV, 2 * angles, depth), jnp.bfloat16),
+        out_shape=pltpu.VMEM((IMG_DEV, 2 * angles, depth), jnp.bfloat16),
         in_specs=[any_space] * 5,
-        out_specs=any_space,
+        out_specs=pl.BlockSpec(memory_space=pltpu.VMEM),
         scratch_shapes=scratch,
         compiler_params=pltpu.CompilerParams(
             collective_id=2, has_side_effects=True, vmem_limit_bytes=VMEM_LIMIT
@@ -919,7 +936,7 @@
         ((pieces, planes) + tile, bf),
         ((pieces, 2, planes - 1, 2) + tile, bf),
         ((2, per * 8, LANES), f32),
-        ((2 * IMG_DEV, angles, depth), bf),
+        ((IMG_DEV, angles, depth), bf),
         ((7, 8, LANES), f32),
         ((5, 8, LANES), f32),
         ((angles, LANES), f32),
@@ -928,11 +945,11 @@
     scratch = [pltpu.VMEM(s, d) for s, d in memory]
     depths = depth // wide
     scratch += [
-        dma((4,)), dma((depths,)), dma((depths,)), dma((depths,)), dma((1,)), dma((1,)),
+        dma((4,)), dma((depths,)), dma((depths + 1,)), dma((depths + 1,)), dma((1,)), dma((1,)),
         dma((1,)), dma((cus, planes)),
         dma((2,)), dma((early + (cus - early) * planes,)),
-        dma((2, 2, planes - 1)), dma((cus, 2, planes - 1)),
-        dma((1,)), dma((1,)), dma((1,)), dma((5,)), dma((5,)),
+        dma((2, 2, planes - 1)), dma((early + 2 * (cus - early), 2, planes - 1)),
+        dma((1,)), dma((1,)), dma((5,)), dma((5,)),
     ]
     return size, scratch, kinds
 

time: 80.8 us -> 79.2 us (0.980)
  local copies, waits for them, and re-layouts: 1.87 us -> 0.8 us
    unnamed x1, local copies, waits for them, and re-layouts: 1.87 us -> 0.8 us
where the time goes in v4:
time: 79.2 us; the launch traced here: 79 us
  Pallas kernels  78.2 us (99%)
  local copies, waits for them, and re-layouts  0.8 us (1%)
    pallas_call x1, Pallas kernels, fused(): pl.pallas_call(functools.partial(fused_kernel, (planes, grp, kinds)), out...  78.2 us

profile of v4, /device:TPU:0, one launch (start us, length us, event | category | flops | bytes accessed | tf_op | source)
XLA Modules:
  0.0 79.0 jit_solution(2678207396829552235)
XLA Ops:
  0.0 78.2 %calibrated_stack.1 = bf16[4,128,512]{2,1,0:T(8,128)(2,1)S(1)} custom-call(bf16[96,2,32,512]{3,2,1,0:T(8,128)(2,1)} %bitcast.5, s32[64,192]{1,0:T(8,128)} %bitcast.6, s32[1,96]{1,0:T(1,128)} %bitcast.8, s32[1,96]{1,0:T(1,128)} %bitcast.9, bf16[32,64]{1,0:T(8,128)(2,1)} %bitcast.7), custom_call_target="tpu_custom_call" | custom-call | tf_op jit(solution)/shard_map/calibrated_stack/pallas_call | solution.py:892
  78.2 0.8 %copy.7 = bf16[4,128,512]{2,1,0:T(8,128)(2,1)} copy(bf16[4,128,512]{2,1,0:T(8,128)(2,1)S(1)} %calibrated_stack.1) | data formatting | bytes 1048576

commit v5 on v4

--- a/solution.py
+++ b/solution.py
@@ -796,7 +796,7 @@
         "slant": slant, "stack": stack, "start": start, "first": first, "second": second,
         "tick": tick, "third": third, "finish": finish, "moments": moments,
     }
-    for _, action in sorted(schedule(planes, kinds), key=lambda e: e[0]):
+    for action in ordered(planes, kinds):
         run[action[0]](*action[1:])
 
     meta.wait_send()
@@ -836,6 +836,49 @@
 
 def far_first(planes):
     return [planes - 1 - i // 2 if i % 2 == 0 else i // 2 for i in range(planes)]
+
+
+ORDERS = {
+    (4, 5, 3): (
+        ("slant", 0, 0), ("slant", 1, 0), ("slant", 0, 1, (0,)), ("stack", 0, (0,)), ("start", 0, (0,)),
+        ("slant", 0, 1, (1,)), ("stack", 0, (1,)), ("start", 0, (1,)), ("slant", 1, 1), ("stack", 1),
+        ("start", 1), ("slant", 3, 0), ("slant", 3, 1), ("first", 0, 3), ("tick", 0, 1, 0),
+        ("first", 0, 0), ("tick", 0, 1, 1), ("stack", 3), ("first", 0, 2), ("start", 3), ("first", 0, 1),
+        ("first", 1, 3), ("slant", 2, 0), ("slant", 2, 1), ("stack", 2), ("start", 2), ("slant", 4, 0),
+        ("tick", 0, 2, 0), ("first", 1, 0), ("tick", 0, 2, 1), ("first", 1, 1), ("slant", 5, 0),
+        ("tick", 1, 1, 1), ("first", 1, 2), ("slant", 4, 1), ("stack", 4), ("slant", 6, 0), ("start", 4),
+        ("slant", 6, 1), ("stack", 6), ("tick", 1, 2, 1), ("first", 3, 3), ("slant", 5, 1),
+        ("tick", 1, 1, 0), ("stack", 5), ("start", 5), ("first", 3, 0), ("first", 2, 0), ("tick", 2, 1, 1),
+        ("first", 2, 2), ("first", 2, 3), ("first", 4, 0), ("start", 6), ("tick", 2, 1, 0),
+        ("tick", 0, 3, 1), ("first", 4, 3), ("first", 4, 1), ("first", 2, 1), ("tick", 4, 1, 0),
+        ("slant", 7, 0), ("tick", 2, 2, 0), ("first", 6, 3), ("tick", 4, 1, 1), ("tick", 1, 3, 1),
+        ("first", 5, 3), ("tick", 3, 1, 0), ("first", 4, 2), ("first", 3, 1), ("slant", 7, 1),
+        ("first", 5, 0), ("first", 6, 0), ("first", 5, 2), ("moments", 0), ("tick", 0, 3, 0),
+        ("moments", 1), ("tick", 3, 1, 1), ("stack", 7), ("start", 7), ("tick", 2, 2, 1),
+        ("tick", 1, 2, 0), ("moments", 2), ("second", 5, 3), ("tick", 3, 2, 1), ("second", 6, 3),
+        ("first", 3, 2), ("tick", 1, 3, 0), ("tick", 4, 2, 1), ("second", 5, 2), ("first", 5, 1),
+        ("first", 7, 3), ("first", 7, 0), ("second", 6, 0), ("tick", 4, 2, 0), ("tick", 5, 1, 0),
+        ("second", 5, 0), ("tick", 5, 1, 1), ("first", 7, 1), ("moments", 3), ("first", 6, 1),
+        ("first", 7, 2), ("second", 5, 1), ("second", 7, 3), ("tick", 3, 2, 0), ("tick", 6, 1, 1),
+        ("first", 6, 2), ("tick", 2, 3, 1), ("second", 7, 0), ("tick", 6, 1, 0), ("moments", 4),
+        ("tick", 2, 3, 0), ("third", 2), ("third", 1), ("tick", 3, 3, 1), ("tick", 7, 1, 1),
+        ("tick", 7, 1, 0), ("tick", 5, 2, 1), ("second", 7, 1), ("tick", 5, 2, 0), ("tick", 4, 3, 1),
+        ("second", 6, 1), ("tick", 4, 3, 0), ("third", 0), ("second", 7, 2), ("moments", 5),
+        ("tick", 6, 2, 1), ("third", 4), ("second", 6, 2), ("tick", 7, 2, 0), ("tick", 7, 2, 1),
+        ("tick", 3, 3, 0), ("third", 3), ("tick", 6, 2, 0), ("tick", 6, 3, 1), ("tick", 5, 3, 1),
+        ("moments", 6), ("moments", 7), ("tick", 7, 3, 0), ("finish", 4), ("finish", 2), ("finish", 0),
+        ("tick", 5, 3, 0), ("finish", 3), ("finish", 1), ("tick", 7, 3, 1), ("finish", 7), ("finish", 5),
+        ("tick", 6, 3, 0), ("finish", 6),
+    ),
+}
+
+
+def ordered(planes, kinds):
+    early = kinds.count("zv")
+    plan = ORDERS.get((planes, early, len(kinds) - early))
+    if plan is None:
+        plan = [action for _, action in sorted(schedule(planes, kinds), key=lambda e: e[0])]
+    return plan
 
 
 def schedule(planes, kinds):

time: 79.2 us -> 76.2 us (0.962)
  Pallas kernels: 78.2 us -> 75.2 us
    pallas_call x1, Pallas kernels: 78.2 us -> 75.2 us  [fused(): pl.pallas_call(functools.partial(fused_kernel, (planes, grp, kinds)), out...]
where the time goes in v5:
time: 76.2 us; the launch traced here: 76 us
  Pallas kernels  75.2 us (99%)
  local copies, waits for them, and re-layouts  0.8 us (1%)
    pallas_call x1, Pallas kernels, fused(): pl.pallas_call(functools.partial(fused_kernel, (planes, grp, kinds)), out...  75.2 us

profile of v5, /device:TPU:0, one launch (start us, length us, event | category | flops | bytes accessed | tf_op | source)
XLA Modules:
  0.0 76.0 jit_solution(5987930679828010864)
XLA Ops:
  0.0 75.2 %calibrated_stack.1 = bf16[4,128,512]{2,1,0:T(8,128)(2,1)S(1)} custom-call(bf16[96,2,32,512]{3,2,1,0:T(8,128)(2,1)} %bitcast.5, s32[64,192]{1,0:T(8,128)} %bitcast.6, s32[1,96]{1,0:T(1,128)} %bitcast.8, s32[1,96]{1,0:T(1,128)} %bitcast.9, bf16[32,64]{1,0:T(8,128)(2,1)} %bitcast.7), custom_call_target="tpu_custom_call" | custom-call | tf_op jit(solution)/shard_map/calibrated_stack/pallas_call | solution.py:935
  75.2 0.8 %copy.7 = bf16[4,128,512]{2,1,0:T(8,128)(2,1)} copy(bf16[4,128,512]{2,1,0:T(8,128)(2,1)S(1)} %calibrated_stack.1) | data formatting | bytes 1048576

commit v6 on v4

--- a/solution.py
+++ b/solution.py
@@ -796,7 +796,7 @@
         "slant": slant, "stack": stack, "start": start, "first": first, "second": second,
         "tick": tick, "third": third, "finish": finish, "moments": moments,
     }
-    for _, action in sorted(schedule(planes, kinds), key=lambda e: e[0]):
+    for action in ordered(planes, kinds):
         run[action[0]](*action[1:])
 
     meta.wait_send()
@@ -836,6 +836,50 @@
 
 def far_first(planes):
     return [planes - 1 - i // 2 if i % 2 == 0 else i // 2 for i in range(planes)]
+
+
+STEPS = ("slant", "stack", "start", "first", "second", "tick", "third", "finish", "moments")
+ORDERS = {
+    (4, 5, 3): (
+        (0, 0, 0), (0, 1, 0), (0, 0, 1, (0,)), (1, 0, (0,)), (2, 0, (0,)),
+        (0, 0, 1, (1,)), (1, 0, (1,)), (2, 0, (1,)), (0, 1, 1), (1, 1),
+        (2, 1), (0, 3, 0), (0, 3, 1), (3, 0, 3), (5, 0, 1, 0),
+        (3, 0, 0), (5, 0, 1, 1), (1, 3), (3, 0, 2), (2, 3), (3, 0, 1),
+        (3, 1, 3), (0, 2, 0), (0, 2, 1), (1, 2), (2, 2), (0, 4, 0),
+        (5, 0, 2, 0), (3, 1, 0), (5, 0, 2, 1), (3, 1, 1), (0, 5, 0),
+        (5, 1, 1, 1), (3, 1, 2), (0, 4, 1), (1, 4), (0, 6, 0), (2, 4),
+        (0, 6, 1), (1, 6), (5, 1, 2, 1), (3, 3, 3), (0, 5, 1),
+        (5, 1, 1, 0), (1, 5), (2, 5), (3, 3, 0), (3, 2, 0), (5, 2, 1, 1),
+        (3, 2, 2), (3, 2, 3), (3, 4, 0), (2, 6), (5, 2, 1, 0),
+        (5, 0, 3, 1), (3, 4, 3), (3, 4, 1), (3, 2, 1), (5, 4, 1, 0),
+        (0, 7, 0), (5, 2, 2, 0), (3, 6, 3), (5, 4, 1, 1), (5, 1, 3, 1),
+        (3, 5, 3), (5, 3, 1, 0), (3, 4, 2), (3, 3, 1), (0, 7, 1),
+        (3, 5, 0), (3, 6, 0), (3, 5, 2), (8, 0), (5, 0, 3, 0),
+        (8, 1), (5, 3, 1, 1), (1, 7), (2, 7), (5, 2, 2, 1),
+        (5, 1, 2, 0), (8, 2), (4, 5, 3), (5, 3, 2, 1), (4, 6, 3),
+        (3, 3, 2), (5, 1, 3, 0), (5, 4, 2, 1), (4, 5, 2), (3, 5, 1),
+        (3, 7, 3), (3, 7, 0), (4, 6, 0), (5, 4, 2, 0), (5, 5, 1, 0),
+        (4, 5, 0), (5, 5, 1, 1), (3, 7, 1), (8, 3), (3, 6, 1),
+        (3, 7, 2), (4, 5, 1), (4, 7, 3), (5, 3, 2, 0), (5, 6, 1, 1),
+        (3, 6, 2), (5, 2, 3, 1), (4, 7, 0), (5, 6, 1, 0), (8, 4),
+        (5, 2, 3, 0), (6, 2), (6, 1), (5, 3, 3, 1), (5, 7, 1, 1),
+        (5, 7, 1, 0), (5, 5, 2, 1), (4, 7, 1), (5, 5, 2, 0), (5, 4, 3, 1),
+        (4, 6, 1), (5, 4, 3, 0), (6, 0), (4, 7, 2), (8, 5),
+        (5, 6, 2, 1), (6, 4), (4, 6, 2), (5, 7, 2, 0), (5, 7, 2, 1),
+        (5, 3, 3, 0), (6, 3), (5, 6, 2, 0), (5, 6, 3, 1), (5, 5, 3, 1),
+        (8, 6), (8, 7), (5, 7, 3, 0), (7, 4), (7, 2), (7, 0),
+        (5, 5, 3, 0), (7, 3), (7, 1), (5, 7, 3, 1), (7, 7), (7, 5),
+        (5, 6, 3, 0), (7, 6),
+    ),
+}
+
+
+def ordered(planes, kinds):
+    early = kinds.count("zv")
+    plan = ORDERS.get((planes, early, len(kinds) - early))
+    if plan is None:
+        return [action for _, action in sorted(schedule(planes, kinds), key=lambda e: e[0])]
+    return [(STEPS[step[0]],) + step[1:] for step in plan]
 
 
 def schedule(planes, kinds):

time: 79.2 us -> 76.2 us (0.962)
  Pallas kernels: 78.2 us -> 75.2 us
    pallas_call x1, Pallas kernels: 78.2 us -> 75.2 us  [fused(): pl.pallas_call(functools.partial(fused_kernel, (planes, grp, kinds)), out...]
where the time goes in v6:
time: 76.2 us; the launch traced here: 76 us
  Pallas kernels  75.2 us (99%)
  local copies, waits for them, and re-layouts  0.8 us (1%)
    pallas_call x1, Pallas kernels, fused(): pl.pallas_call(functools.partial(fused_kernel, (planes, grp, kinds)), out...  75.2 us

profile of v6, /device:TPU:0, one launch (start us, length us, event | category | flops | bytes accessed | tf_op | source)
XLA Modules:
  0.0 76.0 jit_solution(5987930679828010864)
XLA Ops:
  0.0 75.2 %calibrated_stack.1 = bf16[4,128,512]{2,1,0:T(8,128)(2,1)S(1)} custom-call(bf16[96,2,32,512]{3,2,1,0:T(8,128)(2,1)} %bitcast.5, s32[64,192]{1,0:T(8,128)} %bitcast.6, s32[1,96]{1,0:T(1,128)} %bitcast.8, s32[1,96]{1,0:T(1,128)} %bitcast.9, bf16[32,64]{1,0:T(8,128)(2,1)} %bitcast.7), custom_call_target="tpu_custom_call" | custom-call | tf_op jit(solution)/shard_map/calibrated_stack/pallas_call | solution.py:936
  75.2 0.8 %copy.7 = bf16[4,128,512]{2,1,0:T(8,128)(2,1)} copy(bf16[4,128,512]{2,1,0:T(8,128)(2,1)S(1)} %calibrated_stack.1) | data formatting | bytes 1048576
